TPU v7x, 16 devices: a 4x2x1 block of a 4x4x8 slice. The times are simulated.
16 devices in a mesh: rep: 2 (over y, z), grp: 8 (over x, core).
Axes of the slice: x: 4, y: 2, z: 1, core: 2. Of those that a mesh axis runs over, the one named last changes fastest.
The devices are a block of a 4x4x8 slice.
Arguments:
- x_in: bfloat16 [1024, 4096], P(('rep', 'grp')), parts along dimension 0
- seq_len: int32 [1024], P(('rep', 'grp')), parts along dimension 0
- k_cache: bfloat16 [1024, 512, 2, 128], P(('rep', 'grp')), parts along dimension 0
- v_cache: bfloat16 [1024, 512, 2, 128], P(('rep', 'grp')), parts along dimension 0
- gamma_attn: bfloat16 [4096], replicated
- w_qkv: bfloat16 [4096, 4608], replicated
- b_qkv: bfloat16 [4608], replicated
- w_proj: bfloat16 [4096, 4096], replicated
- gamma_mlp: bfloat16 [4096], replicated
- w_in: bfloat16 [2, 13696, 4096], P(None, 'grp')
- w_out: bfloat16 [13696, 4096], P('grp')
Outputs:
- output 1: bfloat16 [1024, 4096], P(('rep', 'grp')), parts along dimension 0
- output 2: bfloat16 [1024, 512, 2, 128], P(('rep', 'grp')), parts along dimension 0
- output 3: bfloat16 [1024, 512, 2, 128], P(('rep', 'grp')), parts along dimension 0
There are 2 independent parts. A program takes and returns all parts, laid end to end along the dimension named above; an argument that names none is the same for every part.
All inputs are finite; a program needn't handle non-finite values.
Results may differ from a plain program's by a relative error of at most 0.00892782.
Values are sent between devices in bfloat16 or wider.
A program may use at most 768 MiB of HBM per device.

v0:
```python
import jax
import jax.numpy as jnp
from jax import lax
from jax.sharding import PartitionSpec as P

HEAD_DIM = 128
ROPE_BASE = 10000.0
EPS = 1e-5


def rms_norm(vals, gain):
    mean_sq = jnp.mean(vals * vals, axis=-1, keepdims=True)
    return (vals * lax.rsqrt(mean_sq + EPS) * gain.astype(jnp.float32)).astype(jnp.bfloat16)


def rotary(vals, positions):
    rot_dim = HEAD_DIM // 2
    inv_freq = ROPE_BASE ** (-jnp.arange(0, rot_dim, 2, dtype=jnp.float32) / rot_dim)
    angles = positions.astype(jnp.float32)[:, None] * inv_freq[None, :]
    cosine = jnp.cos(angles)[:, None, :]
    sine = jnp.sin(angles)[:, None, :]
    pairs = vals[..., :rot_dim].reshape(vals.shape[:-1] + (rot_dim // 2, 2))
    even_part = pairs[..., 0]
    odd_part = pairs[..., 1]
    rotated = jnp.stack([even_part * cosine - odd_part * sine, odd_part * cosine + even_part * sine], axis=-1)
    return jnp.concatenate([rotated.reshape(vals.shape[:-1] + (rot_dim,)), vals[..., rot_dim:]], axis=-1)


def attention_block(x_in, seq_len, k_cache, v_cache, gamma_attn, w_qkv, b_qkv, w_proj):
    batch_rows, cache_len, kv_heads = k_cache.shape[0], k_cache.shape[1], k_cache.shape[2]
    num_heads = w_proj.shape[0] // HEAD_DIM
    q_width = num_heads * HEAD_DIM
    kv_width = kv_heads * HEAD_DIM
    x_f32 = x_in.astype(jnp.float32)
    normed = rms_norm(x_f32, gamma_attn)
    qkv_proj = jnp.dot(normed, w_qkv, preferred_element_type=jnp.float32) + b_qkv.astype(jnp.float32)
    query_rot = rotary(qkv_proj[:, :q_width].reshape(batch_rows, num_heads, HEAD_DIM), seq_len).astype(jnp.bfloat16)
    key_new = rotary(qkv_proj[:, q_width:q_width + kv_width].reshape(batch_rows, kv_heads, HEAD_DIM), seq_len).astype(jnp.bfloat16)
    value_new = qkv_proj[:, q_width + kv_width:].reshape(batch_rows, kv_heads, HEAD_DIM).astype(jnp.bfloat16)
    positions = jnp.arange(cache_len, dtype=jnp.int32)
    at_len = (positions[None, :] == seq_len[:, None])[:, :, None, None]
    k_out = jnp.where(at_len, key_new[:, None], k_cache)
    v_out = jnp.where(at_len, value_new[:, None], v_cache)
    q_grouped = query_rot.reshape(batch_rows, kv_heads, num_heads // kv_heads, HEAD_DIM)
    attn_scores = jnp.einsum('bgqd,blgd->bgql', q_grouped, k_out, preferred_element_type=jnp.float32) * HEAD_DIM ** -0.5
    visible = (positions[None, :] <= seq_len[:, None])[:, None, None, :]
    attn_probs = jax.nn.softmax(jnp.where(visible, attn_scores, -jnp.inf), axis=-1).astype(jnp.bfloat16)
    context = jnp.einsum('bgql,blgd->bgqd', attn_probs, v_out, preferred_element_type=jnp.float32)
    context = context.astype(jnp.bfloat16).reshape(batch_rows, q_width)
    hidden = x_f32 + jnp.dot(context, w_proj, preferred_element_type=jnp.float32)
    return hidden, k_out, v_out


def solution(mesh):
    row_spec = P(('rep', 'grp'))
    repl_spec = P()

    def local_layer(x_in, seq_len, k_cache, v_cache, gamma_attn, w_qkv, b_qkv, w_proj, gamma_mlp, w_in, w_out):
        hidden, k_out, v_out = attention_block(x_in, seq_len, k_cache, v_cache, gamma_attn, w_qkv, b_qkv, w_proj)
        mlp_in = rms_norm(hidden, gamma_mlp)
        group_rows = lax.all_gather(mlp_in, 'grp', axis=0, tiled=True)
        gate_up = jnp.einsum('bh,cfh->bcf', group_rows, w_in, preferred_element_type=jnp.float32)
        swiglu = (jax.nn.silu(gate_up[:, 0]) * gate_up[:, 1]).astype(jnp.bfloat16)
        part_sum = jnp.dot(swiglu, w_out, preferred_element_type=jnp.float32).astype(jnp.bfloat16)
        mlp_out = lax.psum_scatter(part_sum, 'grp', scatter_dimension=0, tiled=True)
        layer_out = (hidden + mlp_out.astype(jnp.float32)).astype(jnp.bfloat16)
        return layer_out, k_out, v_out

    return jax.shard_map(local_layer, mesh=mesh,
                         in_specs=(row_spec, row_spec, row_spec, row_spec, repl_spec, repl_spec, repl_spec,
                                   repl_spec, repl_spec, P(None, 'grp', None), P('grp', None)),
                         out_specs=(row_spec, row_spec, row_spec), check_vma=False)
```

profile of v0, /device:TPU:113, one launch (start us, length us, event | category | flops | bytes accessed | tf_op | source)
XLA Modules:
  0.0 220.8 jit_solution(5958565234928156811)
XLA Ops:
  7.3 0.7 convert_element_type.59
  7.9 0.8 iota_compare_fusion.1
  8.7 1.2 fusion.19
  9.9 0.7 convert_element_type.56
  10.7 0.7 convert_element_type.58
  11.4 15.4 %convolution_add_fusion = f32[64,4608]{1,0:T(8,128)S(1)} fusion(bf16[4096,4608]{1,0:T(8,128)(2,1)} %param.16, f32[4608]{0:T(1024)S(1)} %convert_element_type.58, bf16[64,4096]{1,0:T(8,128)(2,1)} %param.11, f32[4096]{0:T(1024)S(1)} %convert_element_type.56, f32[64]{0:T(128)S(1)} %add_rsqrt_fusion.1), kind=kOutput, calls=%fused_computation.8 | convolution fusion | flops 2417262592 | bytes 39487744 | tf_op jit(solution)/shard_map/dot_general | solution.py:36
  27.0 0.2 copy.41
  27.4 0.1 multiply_cosine_fusion
  27.9 0.2 slice.89
  28.2 1.1 copy.38
  29.2 0.2 subtract_convert_fusion
  29.4 0.1 pad_maximum_fusion
  29.5 1.1 copy.31
  30.6 46.0 %broadcast_select_fusion.1 = (bf16[64,512,2,128]{3,2,1,0:T(2,128)(2,1)}, bf16[64,512,2,128]{3,2,1,0:T(2,128)(2,1)}) fusion(bf16[64,512,2,128]{3,2,1,0:T(2,128)(2,1)} %param.13, pred[64,512]{1,0:T(8,128)(4,1)S(1)} %get-tuple-element.12, bf16[64,2,128]{2,1,0:T(2,128)(2,1)S(1)} %copy.35, bf16[64,512,2,128]{3,2,1,0:T(2,128)(2,1)} %param.14, ...), kind=kLoop, calls=%fused_computation.2 | loop fusion | flops 16777216 | bytes 67207168 | tf_op jit(solution)/shard_map/jit(_where)/select_n | solution.py:42
  76.6 12.2 %fusion.3 = f32[64,2,16,512]{3,2,1,0:T(8,128)} fusion(bf16[64,512,2,128]{3,2,1,0:T(2,128)(2,1)} %get-tuple-element.7, bf16[64,2,16,64]{3,2,1,0:T(8,128)(2,1)S(1)} %bitcast.41, bf16[64,2,16,64]{3,2,1,0:T(8,128)(2,1)S(1)} %copy.31), kind=kOutput, calls=%fused_computation.5 | convolution fusion | flops 269484032 | bytes 21495808 | tf_op jit(solution)/shard_map/bgqd,blgd->bgql/dot_general | solution.py:45
  88.8 5.1 %fusion.34 = (f32[64,2,16]{2,1,0:T(2,128)S(1)}, f32[64,2,16,512]{3,2,1,0:T(8,128)S(1)}) fusion(f32[64,2,16,512]{3,2,1,0:T(8,128)} %fusion.3, pred[64,512]{1,0:T(8,128)(4,1)S(1)} %get-tuple-element.11), kind=kOutput, calls=%fused_computation.63 | output fusion | flops 6291967 | bytes 8429568 | tf_op jit(solution)/shard_map/sub | solution.py:47
  93.9 8.4 %fusion.16 = bf16[64,2,16,128]{3,2,1,0:T(8,128)(2,1)S(1)} fusion(bf16[64,512,2,128]{3,2,1,0:T(2,128)(2,1)} %get-tuple-element.8, f32[64,2,16,512]{3,2,1,0:T(8,128)S(1)} %get-tuple-element.14, f32[64,2,16]{2,1,0:T(2,128)S(1)} %get-tuple-element.13), kind=kOutput, calls=%fused_computation.27 | convolution fusion | flops 270794752 | bytes 21504000 | tf_op jit(solution)/shard_map/bgql,blgd->bgqd/dot_general | solution.py:48
  102.4 13.8 %multiply_reduce_fusion = (f32[64]{0:T(128)S(1)}, f32[64,4096]{1,0:T(8,128)S(1)}) fusion(bf16[4096,4096]{1,0:T(8,128)(2,1)} %param.18, bf16[8,8,32,128]{3,2,1,0:T(8,128)(2,1)S(1)} %bitcast.43, bf16[64,4096]{1,0:T(8,128)(2,1)S(1)} %copy-done), kind=kOutput, calls=%fused_computation.35 | convolution fusion | flops 2148532224 | bytes 35651840 | tf_op jit(solution)/shard_map/dot_general | solution.py:50
  116.2 1.0 multiply_convert_fusion
  117.3 31.1 %all-gather.2.cloned.1.call-done = bf16[512,4096]{1,0:T(8,128)(2,1)} async-done(((bf16[64,4096]{1,0:T(8,128)(2,1)}), bf16[512,4096]{1,0:T(8,128)(2,1)}) %all-gather.2.cloned.1.call-update) | async-done | bytes 4194320 | tf_op jit(solution)/shard_map/all_gather | solution.py:61
  148.4 19.5 %fusion.5 = f32[512,2,1712]{0,2,1:T(8,128)S(1)} fusion(bf16[2,1712,4096]{2,1,0:T(8,128)(2,1)} %param.20, bf16[512,4096]{1,0:T(8,128)(2,1)} %all-gather.2.cloned.1.call-done), kind=kOutput, calls=%fused_computation.10 | convolution fusion | flops 14361296896 | bytes 39256064 | tf_op jit(solution)/shard_map/bh,cfh->bcf/dot_general | solution.py:62
  167.9 13.4 %convolution_convert_fusion = bf16[512,4096]{1,0:T(8,128)(2,1)} fusion(bf16[1712,4096]{1,0:T(8,128)(2,1)} %param.21, f32[512,2,1712]{0,2,1:T(8,128)S(1)} %fusion.5), kind=kOutput, calls=%fused_computation.7 | convolution fusion | flops 7188004864 | bytes 25231360 | tf_op jit(solution)/shard_map/dot_general | solution.py:64
  181.4 30.7 %reduce-scatter.2.cloned.1.call-done = bf16[64,4096]{1,0:T(8,128)(2,1)} async-done(((bf16[512,4096]{1,0:T(8,128)(2,1)}), bf16[64,4096]{1,0:T(8,128)(2,1)}) %reduce-scatter.2.cloned.1.call-update) | async-done | bytes 524304 | tf_op jit(solution)/shard_map/reduce_scatter | solution.py:65
  212.0 1.9 add_convert_fusion
  (25 shorter events, 1.0 us)
Async XLA Ops:
  7.2 141.2 %all-gather.2.cloned.1.call-start = ((), (), s32[]{:S(2)}) async-start(), calls=%async_computation.1 | async-start | bytes 4718592 | tf_op jit(solution)/shard_map/all_gather | solution.py:61
  11.4 15.5 %copy-start.1 = (bf16[4096]{0:T(1024)(128)(2,1)S(1)}, bf16[4096]{0:T(1024)(128)(2,1)}, u32[]{:S(2)}) copy-start(bf16[4096]{0:T(1024)(128)(2,1)} %param.19) | copy-start | bytes 24580
  93.9 8.4 %copy-start = (bf16[64,4096]{1,0:T(8,128)(2,1)S(1)}, bf16[64,4096]{1,0:T(8,128)(2,1)}, u32[]{:S(2)}) copy-start(bf16[64,4096]{1,0:T(8,128)(2,1)} %param.11) | copy-start | bytes 1572868
  117.2 94.8 %reduce-scatter.2.cloned.1.call-start = ((), (), s32[]{:S(2)}) async-start(), calls=%async_computation.2 | async-start | bytes 4718592 | tf_op jit(solution)/shard_map/reduce_scatter | solution.py:65
Sparse Core Ops, SparseCore 0:
  117.3 31.0 all-gather.1
  181.5 30.4 reduce-scatter.1
where the time goes:
time: 224 us; the launch traced here: 221 us
  matrix products  82.7 us (37%)
  waiting for transfers between devices  61.9 us (28%)
  other arithmetic  58.8 us (26%)
  between operations  14.3 us (6%)
  local copies, waits for them, and re-layouts  3.01 us (1%)
    select_n x1, other arithmetic, attention_block(): k_out = jnp.where(at_len, key_new[:, None], k_cache)  46 us
    all_gather x1, waiting for transfers between devices, local_layer(): group_rows = lax.all_gather(mlp_in, 'grp', axis=0, tiled=True)  31.1 us
    reduce_scatter x1, waiting for transfers between devices, local_layer(): mlp_out = lax.psum_scatter(part_sum, 'grp', scatter_dimension=0, tiled=True)  30.7 us
    dot_general x1, matrix products, local_layer(): jnp.einsum('bh,cfh->bcf', group_rows, w_in, preferred_element_type=jnp.fl...  19.5 us
    dot_general x1, matrix products, attention_block(): jnp.dot(normed, w_qkv, preferred_element_type=jnp.float32)  15.4 us
    dot_general x1, matrix products, attention_block(): jnp.dot(context, w_proj, preferred_element_type=jnp.float32)  13.8 us
    dot_general x1, matrix products, local_layer(): jnp.dot(swiglu, w_out, preferred_element_type=jnp.float32)  13.4 us
    dot_general x1, matrix products, attention_block(): jnp.einsum('bgqd,blgd->bgql', q_grouped, k_out, preferred_element_type=jn...  12.2 us
  transfers between devices with their start and end apart: 2, of which 2 were waited for; matrix products, arithmetic and copies ran while one was open for 0% of the time, Pallas kernels for 0%

commit v1 on v0

v1 whole, which is shorter than its diff:
```python
import functools

import jax
import jax.numpy as jnp
from jax import lax
from jax.experimental import pallas as pl
from jax.experimental.pallas import tpu as pltpu
from jax.sharding import PartitionSpec as P

HEAD_DIM = 128
ROT_DIM = HEAD_DIM // 2
ROPE_BASE = 10000.0
EPS = 1e-5
F32 = jnp.float32
BF16 = jnp.bfloat16

TN = 512
NW = 4
SG = 4
NS = 8
LAG = 3


def rope_tables(seq_len):
    dim = jnp.arange(HEAD_DIM, dtype=jnp.int32)
    freq = ROPE_BASE ** (-(dim - dim % 2).astype(F32) / ROT_DIM)
    freq = jnp.where(dim < ROT_DIM, freq, 0.0)
    angles = seq_len.astype(F32)[:, None] * freq[None, :]
    sign = jnp.where(dim % 2 == 0, -1.0, 1.0).astype(F32)
    return jnp.cos(angles), jnp.sin(angles) * sign[None, :]


def norm(vals, gain):
    mean_sq = jnp.mean(vals * vals, axis=-1, keepdims=True)
    return (vals * lax.rsqrt(mean_sq + EPS) * gain.astype(F32)).astype(BF16)


def attention_kernel(len_ref, x_ref, cos_ref, sin_ref, ga_ref, b_ref, gm_ref, kc, vc, wq, wp,
                     m_ref, h_ref, ko, vo,
                     wbuf, kbuf, vbuf, nbuf, qh, qs, kn, vn, cb, colpos, wsem, insem, outsem):
    rows = x_ref.shape[0]
    heads = qh.shape[0]
    q_tiles = heads * HEAD_DIM // TN
    p_tiles = wp.shape[1] // TN
    groups = rows // SG
    per_tile = TN // HEAD_DIM
    span = kbuf.shape[2]

    def q_copy(tile):
        slot = lax.rem(tile, NW)
        cols = pl.ds(pl.multiple_of(tile * TN, TN), TN)
        return pltpu.make_async_copy(wq.at[:, cols], wbuf.at[slot], wsem.at[slot])

    def p_copy(tile):
        slot = lax.rem(tile, NW)
        cols = pl.ds(pl.multiple_of(tile * TN, TN), TN)
        return pltpu.make_async_copy(wp.at[:, cols], wbuf.at[slot], wsem.at[slot])

    def cache_in(group):
        slot = lax.rem(group, NS)
        seqs = pl.ds(group * SG, SG)
        return (pltpu.make_async_copy(kc.at[seqs], kbuf.at[slot], insem.at[slot, 0]),
                pltpu.make_async_copy(vc.at[seqs], vbuf.at[slot], insem.at[slot, 1]))

    def cache_out(group):
        slot = lax.rem(group, NS)
        seqs = pl.ds(group * SG, SG)
        return (pltpu.make_async_copy(kbuf.at[slot], ko.at[seqs], outsem.at[slot, 0]),
                pltpu.make_async_copy(vbuf.at[slot], vo.at[seqs], outsem.at[slot, 1]))

    for t in range(NW):
        q_copy(t).start()

    row_id = lax.broadcasted_iota(jnp.int32, (heads, span), 0)
    col_id = lax.broadcasted_iota(jnp.int32, (heads, span), 1)
    kv_of_row = row_id // (heads // 2)
    colpos[...] = jnp.where((col_id & 1) == kv_of_row, col_id >> 1, span)

    nbuf[...] = norm(x_ref[...].astype(F32), ga_ref[...])

    lane = lax.broadcasted_iota(jnp.int32, (rows, HEAD_DIM), 1)
    even = (lane & 1) == 0

    def rope(v):
        swapped = jnp.where(even, pltpu.roll(v, HEAD_DIM - 1, 1), pltpu.roll(v, 1, 1))
        return v * cos_ref[...] + swapped * sin_ref[...]

    def qkv_tile(tile):
        q_copy(tile).wait()
        cols = pl.ds(pl.multiple_of(tile * TN, TN), TN)
        out = jnp.dot(nbuf[...], wbuf[lax.rem(tile, NW)], preferred_element_type=F32)
        return out + b_ref[:, cols].astype(F32)

    def q_step(tile, carry):
        out = qkv_tile(tile)
        for i in range(per_tile):
            qh[tile * per_tile + i] = rope(out[:, i * HEAD_DIM:(i + 1) * HEAD_DIM])

        @pl.when(tile + NW < q_tiles + 1)
        def _():
            q_copy(tile + NW).start()

        @pl.when(tile + NW >= q_tiles + 1)
        def _():
            first = (tile + NW - q_tiles - 1) * 2
            for g in range(2):
                for c in cache_in(first + g):
                    c.start()
        return carry

    lax.fori_loop(0, q_tiles, q_step, 0)
    out = qkv_tile(q_tiles)
    for g in range(2):
        for c in cache_in((NW - 1) * 2 + g):
            c.start()
    for g in range(2):
        kn[g] = rope(out[:, g * HEAD_DIM:(g + 1) * HEAD_DIM])
        vn[g] = out[:, (2 + g) * HEAD_DIM:(3 + g) * HEAD_DIM]
    for hd in range(heads):
        qs[:, hd, :] = qh[hd]

    sub = lax.broadcasted_iota(jnp.int32, (16, HEAD_DIM), 0)
    scale = HEAD_DIM ** -0.5

    def group_step(group, carry):
        slot = lax.rem(group, NS)
        for c in cache_in(group):
            c.wait()
        for j in range(SG):
            seq = group * SG + j
            length = len_ref[seq]
            start = pl.multiple_of((length // 8) * 16, 16)
            here = (sub >> 1) == (length - (length // 8) * 8)
            for buf, new in ((kbuf, kn), (vbuf, vn)):
                pattern = jnp.where((sub & 1) == 0, new[0, pl.ds(seq, 1), :], new[1, pl.ds(seq, 1), :])
                old = buf[slot, j, pl.ds(start, 16), :].astype(F32)
                buf[slot, j, pl.ds(start, 16), :] = jnp.where(here, pattern, old).astype(BF16)
        for c in cache_out(group):
            c.start()
        for j in range(SG):
            seq = group * SG + j
            length = len_ref[seq]
            scores = lax.dot_general(qs[seq].astype(BF16), kbuf[slot, j], (((1,), (1,)), ((), ())),
                                     preferred_element_type=F32) * scale
            scores = jnp.where(colpos[...] <= length, scores, -jnp.inf)
            top = jnp.max(scores, axis=-1, keepdims=True)
            weights = jnp.exp(scores - top)
            total = jnp.sum(weights, axis=-1, keepdims=True)
            probs = (weights / total).astype(BF16)
            cb[seq] = jnp.dot(probs, vbuf[slot, j], preferred_element_type=F32)

        @pl.when(group >= LAG)
        def _():
            for c in cache_out(group - LAG):
                c.wait()

        @pl.when(jnp.logical_and(group >= LAG, group - LAG + NS < groups))
        def _():
            for c in cache_in(group - LAG + NS):
                c.start()

        @pl.when(group >= groups - NW)
        def _():
            p_copy(group - (groups - NW)).start()
        return carry

    lax.fori_loop(0, groups, group_step, 0)
    for hd in range(heads):
        nbuf[:, hd * HEAD_DIM:(hd + 1) * HEAD_DIM] = cb[:, hd, :].astype(BF16)

    def p_step(tile, carry):
        p_copy(tile).wait()
        cols = pl.ds(pl.multiple_of(tile * TN, TN), TN)
        out = jnp.dot(nbuf[...], wbuf[lax.rem(tile, NW)], preferred_element_type=F32)
        h_ref[:, cols] = x_ref[:, cols].astype(F32) + out

        @pl.when(tile + NW < p_tiles)
        def _():
            p_copy(tile + NW).start()
        return carry

    lax.fori_loop(0, p_tiles, p_step, 0)
    m_ref[...] = norm(h_ref[...], gm_ref[...])
    for g in range(LAG):
        for c in cache_out(groups - LAG + g):
            c.wait()


def attention_block(x_in, seq_len, k_cache, v_cache, gamma_attn, w_qkv, b_qkv, w_proj, gamma_mlp):
    rows, width = x_in.shape
    cache_len, kv_heads = k_cache.shape[1], k_cache.shape[2]
    heads = w_proj.shape[0] // HEAD_DIM
    span = cache_len * kv_heads
    cos, sin = rope_tables(seq_len)
    flat = (rows, span, HEAD_DIM)
    vmem = pl.BlockSpec(memory_space=pltpu.VMEM)
    hbm = pl.BlockSpec(memory_space=pl.ANY)
    m, h, k_out, v_out = pl.pallas_call(
        attention_kernel,
        out_shape=(jax.ShapeDtypeStruct((rows, width), BF16), jax.ShapeDtypeStruct((rows, width), F32),
                   jax.ShapeDtypeStruct(flat, BF16), jax.ShapeDtypeStruct(flat, BF16)),
        in_specs=[pl.BlockSpec(memory_space=pltpu.SMEM)] + [vmem] * 6 + [hbm] * 4,
        out_specs=(vmem, vmem, hbm, hbm),
        scratch_shapes=[
            pltpu.VMEM((NW, width, TN), BF16),
            pltpu.VMEM((NS, SG, span, HEAD_DIM), BF16),
            pltpu.VMEM((NS, SG, span, HEAD_DIM), BF16),
            pltpu.VMEM((rows, width), BF16),
            pltpu.VMEM((heads, rows, HEAD_DIM), F32),
            pltpu.VMEM((rows, heads, HEAD_DIM), F32),
            pltpu.VMEM((kv_heads, rows, HEAD_DIM), F32),
            pltpu.VMEM((kv_heads, rows, HEAD_DIM), F32),
            pltpu.VMEM((rows, heads, HEAD_DIM), F32),
            pltpu.VMEM((heads, span), jnp.int32),
            pltpu.SemaphoreType.DMA((NW,)),
            pltpu.SemaphoreType.DMA((NS, 2)),
            pltpu.SemaphoreType.DMA((NS, 2)),
        ],
        compiler_params=pltpu.CompilerParams(vmem_limit_bytes=56 * 1024 * 1024),
        name='attention_block',
    )(seq_len, x_in, cos, sin, gamma_attn[None, :], b_qkv[None, :], gamma_mlp[None, :],
      k_cache.reshape(flat), v_cache.reshape(flat), w_qkv, w_proj)
    return m, h, k_out.reshape(k_cache.shape), v_out.reshape(v_cache.shape)


def solution(mesh):
    row_spec = P(('rep', 'grp'))
    repl_spec = P()

    def local_layer(x_in, seq_len, k_cache, v_cache, gamma_attn, w_qkv, b_qkv, w_proj, gamma_mlp, w_in, w_out):
        mlp_in, hidden, k_out, v_out = attention_block(
            x_in, seq_len, k_cache, v_cache, gamma_attn, w_qkv, b_qkv, w_proj, gamma_mlp)
        group_rows = lax.all_gather(mlp_in, 'grp', axis=0, tiled=True)
        gate_up = jnp.einsum('bh,cfh->bcf', group_rows, w_in, preferred_element_type=jnp.float32)
        swiglu = (jax.nn.silu(gate_up[:, 0]) * gate_up[:, 1]).astype(jnp.bfloat16)
        part_sum = jnp.dot(swiglu, w_out, preferred_element_type=jnp.float32).astype(jnp.bfloat16)
        mlp_out = lax.psum_scatter(part_sum, 'grp', scatter_dimension=0, tiled=True)
        layer_out = (hidden + mlp_out.astype(jnp.float32)).astype(jnp.bfloat16)
        return layer_out, k_out, v_out

    return jax.shard_map(local_layer, mesh=mesh,
                         in_specs=(row_spec, row_spec, row_spec, row_spec, repl_spec, repl_spec, repl_spec,
                                   repl_spec, repl_spec, P(None, 'grp', None), P('grp', None)),
                         out_specs=(row_spec, row_spec, row_spec), check_vma=False)
```

time: 224 us -> 174 us (0.78)
  other arithmetic: 58.8 us -> 3.41 us
  Pallas kernels: 0 us -> 54.2 us
  matrix products: 82.7 us -> 32.9 us
    pallas_call x0 -> x1, Pallas kernels: none -> 54.2 us  [attention_block(): pl.pallas_call(attention_kernel, out_shape=(jax.ShapeDtypeStruct((rows, w...]
    dot_general x4 -> x0, matrix products: 49.8 us -> none  [the longest x1 15.4 us: attention_block(): jnp.dot(normed, w_qkv, preferred_element_type=jnp.float32)]
    select_n x1, other arithmetic: 46 us -> 0.01 us  [rope_tables(): sign = jnp.where(dim % 2 == 0, -1.0, 1.0).astype(F32)]
    sub x1 -> x0, other arithmetic: 5.13 us -> none  [attention_block(): jax.nn.softmax(jnp.where(visible, attn_scores, -jnp.inf), axis=-1)]
    broadcast_in_dim x0 -> x3, local copies, waits for them, and re-layouts: none -> 3.93 us  [the longest x1 1.31 us: attention_block(): b_qkv[None, :]]
    convert_element_type x5 -> x1, other arithmetic: 3.05 us -> 0.66 us  [rope_tables(): angles = seq_len.astype(F32)[:, None] * freq[None, :]]
where the time goes in v1:
time: 174 us; the launch traced here: 171 us
  waiting for transfers between devices  61.7 us (35%)
  Pallas kernels  54.2 us (31%)
  matrix products  32.9 us (19%)
  between operations  14.1 us (8%)
  local copies, waits for them, and re-layouts  3.93 us (2%)
  other arithmetic  3.41 us (2%)
    pallas_call x1, Pallas kernels, attention_block(): pl.pallas_call(attention_kernel, out_shape=(jax.ShapeDtypeStruct((rows, w...  54.2 us
    all_gather x1, waiting for transfers between devices, local_layer(): group_rows = lax.all_gather(mlp_in, 'grp', axis=0, tiled=True)  31 us
    reduce_scatter x1, waiting for transfers between devices, local_layer(): mlp_out = lax.psum_scatter(part_sum, 'grp', scatter_dimension=0, tiled=True)  30.7 us
    dot_general x1, matrix products, local_layer(): jnp.einsum('bh,cfh->bcf', group_rows, w_in, preferred_element_type=jnp.fl...  19.5 us
    dot_general x1, matrix products, local_layer(): jnp.dot(swiglu, w_out, preferred_element_type=jnp.float32)  13.4 us
  transfers between devices with their start and end apart: 2, of which 2 were waited for; matrix products, arithmetic and copies ran while one was open for 0% of the time, Pallas kernels for 0%

profile of v1, /device:TPU:113, one launch (start us, length us, event | category | flops | bytes accessed | tf_op | source)
XLA Modules:
  0.0 170.6 jit_solution(9942335360321564553)
XLA Ops:
  7.2 0.1 all-gather.2.cloned.1.call-start
  7.3 0.7 convert_element_type.22
  7.9 1.3 broadcast_in_dim.27.ga_ref
  9.2 1.3 broadcast_in_dim.29.gm_ref
  10.5 1.3 broadcast_in_dim.28.b_ref
  11.8 0.8 fusion.6
  12.7 54.2 %attention_block.1 = (bf16[64,4096]{1,0:T(8,128)(2,1)}, f32[64,4096]{1,0:T(8,128)}, bf16[64,1024,128]{2,1,0:T(8,128)(2,1)}, bf16[64,1024,128]{2,1,0:T(8,128)(2,1)}) custom-call(s32[64]{0:T(128)} %len_ref.1, bf16[64,4096]{1,0:T(8,128)(2,1)} %x_ref.1, f32[64,128]{1,0:T(8,128)} %get-tuple-element.12.cos_ref, f32[64,128]{1,0:T(8,128)} %get-tuple-element.11.sin_ref, ...), custom_call_target="tpu_custom_call" | custom-call | tf_op jit(solution)/shard_map/attention_block/pallas_call | solution.py:198
  66.9 0.1 all-gather.2.cloned.1.call-update
  67.0 0.2 reduce-scatter.2.cloned.1.call-start
  67.2 31.0 %all-gather.2.cloned.1.call-done = bf16[512,4096]{1,0:T(8,128)(2,1)} async-done(((bf16[64,4096]{1,0:T(8,128)(2,1)}), bf16[512,4096]{1,0:T(8,128)(2,1)}) %all-gather.2.cloned.1.call-update) | async-done | bytes 4194320 | tf_op jit(solution)/shard_map/all_gather | solution.py:233
  98.2 19.5 %fusion = f32[512,2,1712]{0,2,1:T(8,128)S(1)} fusion(bf16[2,1712,4096]{2,1,0:T(8,128)(2,1)} %param.20, bf16[512,4096]{1,0:T(8,128)(2,1)} %all-gather.2.cloned.1.call-done), kind=kOutput, calls=%fused_computation.1 | convolution fusion | flops 14361296896 | bytes 39256064 | tf_op jit(solution)/shard_map/bh,cfh->bcf/dot_general | solution.py:234
  117.7 0.0 copy-start
  117.7 13.4 %convolution_convert_fusion = bf16[512,4096]{1,0:T(8,128)(2,1)} fusion(bf16[1712,4096]{1,0:T(8,128)(2,1)} %param.21, f32[512,2,1712]{0,2,1:T(8,128)S(1)} %fusion), kind=kOutput, calls=%fused_computation | convolution fusion | flops 7188004864 | bytes 25231360 | tf_op jit(solution)/shard_map/dot_general | solution.py:236
  131.1 0.1 reduce-scatter.2.cloned.1.call-update
  131.2 30.7 %reduce-scatter.2.cloned.1.call-done = bf16[64,4096]{1,0:T(8,128)(2,1)} async-done(((bf16[512,4096]{1,0:T(8,128)(2,1)}), bf16[64,4096]{1,0:T(8,128)(2,1)}) %reduce-scatter.2.cloned.1.call-update) | async-done | bytes 524304 | tf_op jit(solution)/shard_map/reduce_scatter | solution.py:237
  161.8 0.0 copy-done
  161.8 1.9 %add_convert_fusion = bf16[64,4096]{1,0:T(8,128)(2,1)} fusion(f32[64,4096]{1,0:T(8,128)S(1)} %copy-done, bf16[64,4096]{1,0:T(8,128)(2,1)} %reduce-scatter.2.cloned.1.call-done), kind=kLoop, calls=%fused_computation.8 | loop fusion | flops 786432 | bytes 2097152 | tf_op jit(solution)/shard_map/convert_element_type | solution.py:238
  (1 shorter events, 0.0 us)
Async XLA Ops:
  7.2 91.0 %all-gather.2.cloned.1.call-start = ((), (), s32[]{:S(2)}) async-start(), calls=%async_computation.1 | async-start | bytes 4718592 | tf_op jit(solution)/shard_map/all_gather | solution.py:233
  67.0 94.9 %reduce-scatter.2.cloned.1.call-start = ((), (), s32[]{:S(2)}) async-start(), calls=%async_computation.2 | async-start | bytes 4718592 | tf_op jit(solution)/shard_map/reduce_scatter | solution.py:237
  117.7 44.1 %copy-start = (f32[64,4096]{1,0:T(8,128)S(1)}, f32[64,4096]{1,0:T(8,128)}, u32[]{:S(2)}) copy-start(f32[64,4096]{1,0:T(8,128)} %get-tuple-element.7) | copy-start | bytes 3145732
Sparse Core Ops, SparseCore 0:
  67.1 31.0 all-gather.1
  131.3 30.4 reduce-scatter.1

commit v2 on v1

--- a/solution.py
+++ b/solution.py
@@ -222,6 +222,223 @@
       k_cache.reshape(flat), v_cache.reshape(flat), w_qkv, w_proj)
     return m, h, k_out.reshape(k_cache.shape), v_out.reshape(v_cache.shape)
 
+FT = 1024
+HT = 256
+
+
+def mlp_kernel(m_in, h_in, wi, wo, out_ref,
+               rows_all, wib, wob, gbuf, facc, hold, acc, topart, frompart, outbox, from_l, from_r, mid_l, mid_r,
+               wsem, isem, gsend, grecv, psend, precv, bsend, brecv):
+    me = lax.axis_index('grp')
+    chips = lax.axis_size('grp') // 2
+    chip, core = me // 2, me % 2
+    right = lax.rem(chip + 1, chips) * 2 + core
+    left = lax.rem(chip + chips - 1, chips) * 2 + core
+    partner = chip * 2 + 1 - core
+    r = m_in.shape[0]
+    s, g, br = r // 2, 2 * r, 4 * r
+    hidden = wo.shape[0]
+    full = hidden // HT
+    rest = hidden - full * HT
+    hpad = wob.shape[0]
+    tiles = wo.shape[1] // FT
+
+    def w_copy(j):
+        part = pl.ds(pl.multiple_of(j * HT, HT), HT)
+        return pltpu.make_async_copy(wi.at[:, part], wib.at[:, part], wsem.at[j])
+
+    last_in = pltpu.make_async_copy(wi.at[:, pl.ds(full * HT, rest)], wib.at[:, pl.ds(full * HT, rest)], wsem.at[full])
+    m_copy = pltpu.make_async_copy(m_in, rows_all.at[pl.ds(0, r)], isem.at[0])
+    h_copy = pltpu.make_async_copy(h_in, acc, isem.at[1])
+    o_copy = pltpu.make_async_copy(wo, wob.at[pl.ds(0, hidden)], isem.at[2])
+    m_copy.start()
+    for j in range(full):
+        w_copy(j).start()
+    last_in.start()
+    o_copy.start()
+    h_copy.start()
+
+    barrier = pltpu.get_barrier_semaphore()
+    for dev in (right, left, partner):
+        pl.semaphore_signal(barrier, inc=1, device_id={'grp': dev}, device_id_type=pl.DeviceIdType.MESH)
+    pl.semaphore_wait(barrier, 3)
+
+    def remote(src, dst, send, recv, dev):
+        return pltpu.make_async_remote_copy(src_ref=src, dst_ref=dst, send_sem=send, recv_sem=recv,
+                                            device_id={'grp': dev}, device_id_type=pl.DeviceIdType.MESH)
+
+    def gather(n, src, dst, count, dev):
+        return remote(rows_all.at[pl.ds(src, count)], rows_all.at[pl.ds(dst, count)], gsend.at[n], grecv.at[n], dev)
+
+    to_r0 = gather(0, 0, r, s, right)
+    to_l1 = gather(1, s, r + s, s, left)
+    to_r1 = gather(2, s, br + r, s, right)
+    to_l0 = gather(3, 0, br + r + s, s, left)
+    to_p = gather(4, 0, g, r, partner)
+    on_r = gather(5, r, br, s, right)
+    on_l = gather(6, r + s, br + s, s, left)
+    p_l0 = gather(7, r, g + r, s, partner)
+    p_r1 = gather(8, r + s, g + r + s, s, partner)
+    p_l1 = gather(9, br + r, br + g + r, s, partner)
+    p_r0 = gather(10, br + r + s, br + g + r + s, s, partner)
+    p_o0 = gather(11, br, br + g, s, partner)
+    p_o1 = gather(12, br + s, br + g + s, s, partner)
+    gathers = [to_r0, to_l1, to_r1, to_l0, to_p, on_r, on_l, p_l0, p_r1, p_l1, p_r0, p_o0, p_o1]
+
+    m_copy.wait()
+    for c in (to_r0, to_l1, to_p, to_r1, to_l0):
+        c.start()
+    if hpad > hidden:
+        wib[:, hidden:, :] = jnp.zeros((2, hpad - hidden, wib.shape[2]), BF16)
+        wob[hidden:, :] = jnp.zeros((hpad - hidden, wob.shape[1]), BF16)
+
+    to_r0.wait_recv()
+    on_r.start()
+    p_l0.start()
+    to_l1.wait_recv()
+    on_l.start()
+    p_r1.start()
+    for c in (to_p, p_l0, p_r1):
+        c.wait_recv()
+
+    def gate_tile(blk, j):
+        part = pl.ds(pl.multiple_of(j * HT, HT), HT)
+        x = rows_all[pl.ds(blk * br, br)]
+        dims = (((1,), (1,)), ((), ()))
+        gate = lax.dot_general(x, wib[0, part, :], dims, preferred_element_type=F32)
+        up = lax.dot_general(x, wib[1, part, :], dims, preferred_element_type=F32)
+        gbuf[:, part] = (jax.nn.silu(gate) * up).astype(BF16)
+
+    def cols(t):
+        return slice(t * FT, (t + 1) * FT)
+
+    def to_partner(blk, t):
+        return remote(topart.at[t], frompart.at[blk, t], psend.at[blk, t], precv.at[blk, t], partner)
+
+    def out_copy(kind, t):
+        dst = (from_r.at[0, t], from_l.at[1, t], mid_l.at[t], mid_r.at[t], from_l.at[0, t], from_r.at[1, t])[kind]
+        dev = (left, right, right, left, right, left)[kind]
+        return remote(outbox.at[kind, t], dst, bsend.at[kind, t], brecv.at[kind, t], dev)
+
+    def post(kind, t, vals):
+        outbox[kind, t] = vals.astype(BF16)
+        out_copy(kind, t).start()
+
+    def down_tile(blk, t):
+        f = jnp.dot(gbuf[...], wob[:, cols(t)], preferred_element_type=F32)
+        if blk == 1:
+            to_partner(0, t).wait_send()
+        topart[t] = f[g:].astype(BF16)
+        to_partner(blk, t).start()
+        facc[t % 2] = f[:g]
+
+    def finish(blk, t):
+        to_partner(blk, t).wait_recv()
+        total = facc[t % 2] + frompart[blk, t].astype(F32)
+        if blk == 0:
+            acc[:, cols(t)] += total[:r]
+            post(0, t, total[r:r + s])
+            post(1, t, total[r + s:])
+        else:
+            post(2, t, total[:s])
+            post(3, t, total[s:r])
+            hold[t] = total[r:]
+
+    def step0(j, carry):
+        w_copy(j).wait()
+        gate_tile(0, j)
+        return carry
+
+    lax.fori_loop(0, full, step0, 0)
+    if rest:
+        last_in.wait()
+        gate_tile(0, full)
+    to_r1.wait_recv()
+    p_l1.start()
+    to_l0.wait_recv()
+    p_r0.start()
+    o_copy.wait()
+    h_copy.wait()
+    for t in range(tiles):
+        down_tile(0, t)
+        if t:
+            finish(0, t - 1)
+        if t == tiles - 2:
+            on_r.wait_recv()
+            p_o0.start()
+            on_l.wait_recv()
+            p_o1.start()
+    for c in (p_l1, p_r0, p_o0, p_o1):
+        c.wait_recv()
+
+    gate_tile(1, 0)
+    finish(0, tiles - 1)
+
+    def step1(j, carry):
+        gate_tile(1, j)
+        return carry
+
+    lax.fori_loop(1, hpad // HT, step1, 0)
+    for t in range(tiles):
+        down_tile(1, t)
+        if t:
+            finish(1, t - 1)
+    finish(1, tiles - 1)
+    for t in range(tiles):
+        out_copy(2, t).wait_recv()
+        post(4, t, hold[t, s:] + mid_l[t].astype(F32))
+        out_copy(3, t).wait_recv()
+        post(5, t, hold[t, :s] + mid_r[t].astype(F32))
+    for t in range(tiles):
+        for kind in (0, 1, 4, 5):
+            out_copy(kind, t).wait_recv()
+        for half in range(2):
+            part = slice(half * s, (half + 1) * s)
+            total = acc[part, cols(t)] + (from_l[half, t].astype(F32) + from_r[half, t].astype(F32))
+            out_ref[part, cols(t)] = total.astype(BF16)
+    for c in gathers:
+        c.wait_send()
+    for t in range(tiles):
+        to_partner(1, t).wait_send()
+        for kind in range(6):
+            out_copy(kind, t).wait_send()
+
+
+def mlp_block(m, h, w_in, w_out):
+    rows, width = m.shape
+    hidden = w_out.shape[0]
+    hpad = -(-hidden // HT) * HT
+    tiles = width // FT
+    half, group, block = rows // 2, 2 * rows, 4 * rows
+    hbm = pl.BlockSpec(memory_space=pl.ANY)
+    dma = pltpu.SemaphoreType.DMA
+    return pl.pallas_call(
+        mlp_kernel,
+        out_shape=jax.ShapeDtypeStruct((rows, width), BF16),
+        in_specs=[hbm] * 4,
+        out_specs=pl.BlockSpec(memory_space=pltpu.VMEM),
+        scratch_shapes=[
+            pltpu.VMEM((2 * block, width), BF16),
+            pltpu.VMEM((2, hpad, width), BF16),
+            pltpu.VMEM((hpad, width), BF16),
+            pltpu.VMEM((block, hpad), BF16),
+            pltpu.VMEM((2, group, FT), F32),
+            pltpu.VMEM((tiles, rows, FT), F32),
+            pltpu.VMEM((rows, width), F32),
+            pltpu.VMEM((tiles, group, FT), BF16),
+            pltpu.VMEM((2, tiles, group, FT), BF16),
+            pltpu.VMEM((6, tiles, half, FT), BF16),
+            pltpu.VMEM((2, tiles, half, FT), BF16),
+            pltpu.VMEM((2, tiles, half, FT), BF16),
+            pltpu.VMEM((tiles, half, FT), BF16),
+            pltpu.VMEM((tiles, half, FT), BF16),
+            dma((hpad // HT,)), dma((3,)), dma((13,)), dma((13,)),
+            dma((2, tiles)), dma((2, tiles)), dma((6, tiles)), dma((6, tiles)),
+        ],
+        compiler_params=pltpu.CompilerParams(vmem_limit_bytes=67043328, collective_id=0, has_side_effects=True),
+        name='mlp_block',
+    )(m, h, w_in, w_out)
+
 
 def solution(mesh):
     row_spec = P(('rep', 'grp'))
@@ -230,12 +447,7 @@
     def local_layer(x_in, seq_len, k_cache, v_cache, gamma_attn, w_qkv, b_qkv, w_proj, gamma_mlp, w_in, w_out):
         mlp_in, hidden, k_out, v_out = attention_block(
             x_in, seq_len, k_cache, v_cache, gamma_attn, w_qkv, b_qkv, w_proj, gamma_mlp)
-        group_rows = lax.all_gather(mlp_in, 'grp', axis=0, tiled=True)
-        gate_up = jnp.einsum('bh,cfh->bcf', group_rows, w_in, preferred_element_type=jnp.float32)
-        swiglu = (jax.nn.silu(gate_up[:, 0]) * gate_up[:, 1]).astype(jnp.bfloat16)
-        part_sum = jnp.dot(swiglu, w_out, preferred_element_type=jnp.float32).astype(jnp.bfloat16)
-        mlp_out = lax.psum_scatter(part_sum, 'grp', scatter_dimension=0, tiled=True)
-        layer_out = (hidden + mlp_out.astype(jnp.float32)).astype(jnp.bfloat16)
+        layer_out = mlp_block(mlp_in, hidden, w_in, w_out)
         return layer_out, k_out, v_out
 
     return jax.shard_map(local_layer, mesh=mesh,

time: 174 us -> 122 us (0.70); the launches traced: 171 us -> 122 us
  waiting for transfers between devices: 61.7 us -> 0 us
  Pallas kernels: 54.2 us -> 114 us
  matrix products: 32.9 us -> 0 us
  between operations: 14.1 us -> 0.65 us
  other arithmetic: 3.41 us -> 1.5 us
  local copies, waits for them, and re-layouts: 3.93 us -> 5.79 us
    pallas_call x0 -> x1, Pallas kernels: none -> 59.9 us  [mlp_block(): pl.pallas_call(mlp_kernel, out_shape=jax.ShapeDtypeStruct((rows, width),...]
    dot_general x2 -> x0, matrix products: 32.9 us -> none  [the longest x1 19.5 us: local_layer(): jnp.einsum('bh,cfh->bcf', group_rows, w_in, preferred_element_type=jnp.fl...]
    all_gather x1 -> x0, waiting for transfers between devices: 31 us -> none  [local_layer(): group_rows = lax.all_gather(mlp_in, 'grp', axis=0, tiled=True)]
    reduce_scatter x1 -> x0, waiting for transfers between devices: 30.7 us -> none  [local_layer(): mlp_out = lax.psum_scatter(part_sum, 'grp', scatter_dimension=0, tiled=True)]
    convert_element_type x1 -> x0, other arithmetic: 1.92 us -> none  [local_layer(): layer_out = (hidden + mlp_out.astype(jnp.float32)).astype(jnp.bfloat16)]
    unnamed x2 -> x1, local copies, waits for them, and re-layouts: 0.01 us -> 1.87 us
  transfers between devices with their start and end apart: 2 -> 0, of which waited for: 2 -> 0; matrix products, arithmetic and copies ran while one was open for 0% -> 0% of each run, Pallas kernels for 0% -> 0%
where the time goes in v2:
time: 122 us
  Pallas kernels  114 us (93%)
  local copies, waits for them, and re-layouts  5.79 us (5%)
  other arithmetic  1.5 us (1%)
    pallas_call x1, Pallas kernels, mlp_block(): pl.pallas_call(mlp_kernel, out_shape=jax.ShapeDtypeStruct((rows, width),...  59.9 us
    pallas_call x1, Pallas kernels, attention_block(): pl.pallas_call(attention_kernel, out_shape=(jax.ShapeDtypeStruct((rows, w...  54.2 us

profile of v2, /device:TPU:113, one launch (start us, length us, event | category | flops | bytes accessed | tf_op | source)
XLA Modules:
  0.0 122.0 jit_solution(15811781650900605777)
XLA Ops:
  0.6 0.7 convert_element_type.10
  1.3 1.3 %broadcast_in_dim.27.ga_ref = bf16[1,4096]{1,0:T(2,128)(2,1)} reshape(bf16[4096]{0:T(1024)(128)(2,1)} %param.15) | data formatting | bytes 16384 | tf_op jit(solution)/shard_map/broadcast_in_dim | solution.py:221
  2.6 1.3 %broadcast_in_dim.29.gm_ref = bf16[1,4096]{1,0:T(2,128)(2,1)} reshape(bf16[4096]{0:T(1024)(128)(2,1)} %param.19) | data formatting | bytes 16384 | tf_op jit(solution)/shard_map/broadcast_in_dim | solution.py:221
  3.9 1.3 %broadcast_in_dim.28.b_ref = bf16[1,4608]{1,0:T(2,128)(2,1)} reshape(bf16[4608]{0:T(1024)(128)(2,1)} %param.17) | data formatting | bytes 18432 | tf_op jit(solution)/shard_map/broadcast_in_dim | solution.py:221
  5.2 0.8 fusion
  6.0 54.2 %attention_block.1 = (bf16[64,4096]{1,0:T(8,128)(2,1)}, f32[64,4096]{1,0:T(8,128)}, bf16[64,1024,128]{2,1,0:T(8,128)(2,1)}, bf16[64,1024,128]{2,1,0:T(8,128)(2,1)}) custom-call(s32[64]{0:T(128)} %len_ref.1, bf16[64,4096]{1,0:T(8,128)(2,1)} %x_ref.1, f32[64,128]{1,0:T(8,128)} %get-tuple-element.12.cos_ref, f32[64,128]{1,0:T(8,128)} %get-tuple-element.11.sin_ref, ...), custom_call_target="tpu_custom_call" | custom-call | tf_op jit(solution)/shard_map/attention_block/pallas_call | solution.py:198
  60.3 59.9 %mlp_block.1 = bf16[64,4096]{1,0:T(8,128)(2,1)} custom-call(bf16[64,4096]{1,0:T(8,128)(2,1)} %get-tuple-element.7.m_in, f32[64,4096]{1,0:T(8,128)} %get-tuple-element.8.h_in, bf16[2,1712,4096]{2,1,0:T(8,128)(2,1)} %wi.1, bf16[1712,4096]{1,0:T(8,128)(2,1)} %wo.1), custom_call_target="tpu_custom_call" | custom-call | tf_op jit(solution)/shard_map/mlp_block/pallas_call | solution.py:415
  120.1 1.9 %copy.15 = bf16[64,4096]{1,0:T(8,128)(2,1)} copy(bf16[64,4096]{1,0:T(8,128)(2,1)} %mlp_block.1) | data formatting | bytes 1048576
  (1 shorter events, 0.0 us)

commit v3 on v2

v3 whole, which is shorter than its diff:
```python
import math

import jax
import jax.numpy as jnp
from jax import lax
from jax.experimental import pallas as pl
from jax.experimental.pallas import tpu as pltpu
from jax.sharding import PartitionSpec as P

HEAD_DIM = 128
ROT_DIM = HEAD_DIM // 2
ROPE_BASE = 10000.0
EPS = 1e-5
F32 = jnp.float32
BF16 = jnp.bfloat16

TN = 512
NW = 4
SG = 4
NS = 8
LAG = 3


def norm(vals, gain):
    mean_sq = jnp.mean(vals * vals, axis=-1, keepdims=True)
    return (vals * lax.rsqrt(mean_sq + EPS) * gain.astype(F32)).astype(BF16)


def attention_kernel(len_ref, x_ref, ga_ref, b_ref, kc, vc, wq,
                     ctx_ref, ko, vo,
                     wbuf, kbuf, vbuf, nbuf, bias, cos, sin, qh, qs, kn, vn, cb, colpos, wsem, insem, outsem):
    rows = x_ref.shape[0]
    heads = qh.shape[0]
    q_tiles = heads * HEAD_DIM // TN
    groups = rows // SG
    per_tile = TN // HEAD_DIM
    span = kbuf.shape[2]

    def q_copy(tile):
        slot = lax.rem(tile, NW)
        cols = pl.ds(pl.multiple_of(tile * TN, TN), TN)
        return pltpu.make_async_copy(wq.at[:, cols], wbuf.at[slot], wsem.at[slot])

    def cache_in(group):
        slot = lax.rem(group, NS)
        seqs = pl.ds(group * SG, SG)
        return (pltpu.make_async_copy(kc.at[seqs], kbuf.at[slot], insem.at[slot, 0]),
                pltpu.make_async_copy(vc.at[seqs], vbuf.at[slot], insem.at[slot, 1]))

    def cache_out(group):
        slot = lax.rem(group, NS)
        seqs = pl.ds(group * SG, SG)
        return (pltpu.make_async_copy(kbuf.at[slot], ko.at[seqs], outsem.at[slot, 0]),
                pltpu.make_async_copy(vbuf.at[slot], vo.at[seqs], outsem.at[slot, 1]))

    for t in range(NW):
        q_copy(t).start()

    row_id = lax.broadcasted_iota(jnp.int32, (heads, span), 0)
    col_id = lax.broadcasted_iota(jnp.int32, (heads, span), 1)
    kv_of_row = row_id // (heads // 2)
    colpos[...] = jnp.where((col_id & 1) == kv_of_row, col_id >> 1, span)

    nbuf[...] = norm(x_ref[...].astype(F32), ga_ref[...].astype(F32)[None, :])
    bias[...] = b_ref[...].astype(F32)[None, :]
    dim = lax.broadcasted_iota(jnp.int32, (1, HEAD_DIM), 1)
    freq = jnp.exp((dim - (dim & 1)).astype(F32) * (-math.log(ROPE_BASE) / ROT_DIM))
    freq = jnp.where(dim < ROT_DIM, freq, 0.0)
    for i in range(rows):
        cos[i:i + 1, :] = len_ref[i].astype(F32) * freq
    angles = cos[...]
    sign = jnp.where((dim & 1) == 0, -1.0, 1.0)
    cos[...] = jnp.cos(angles)
    sin[...] = jnp.sin(angles) * sign

    lane = lax.broadcasted_iota(jnp.int32, (rows, HEAD_DIM), 1)
    even = (lane & 1) == 0

    def rope(v):
        swapped = jnp.where(even, pltpu.roll(v, HEAD_DIM - 1, 1), pltpu.roll(v, 1, 1))
        return v * cos[...] + swapped * sin[...]

    def qkv_tile(tile):
        q_copy(tile).wait()
        cols = pl.ds(pl.multiple_of(tile * TN, TN), TN)
        out = jnp.dot(nbuf[...], wbuf[lax.rem(tile, NW)], preferred_element_type=F32)
        return out + bias[:, cols]

    def q_step(tile, carry):
        out = qkv_tile(tile)
        for i in range(per_tile):
            qh[tile * per_tile + i] = rope(out[:, i * HEAD_DIM:(i + 1) * HEAD_DIM])

        @pl.when(tile + NW < q_tiles + 1)
        def _():
            q_copy(tile + NW).start()

        @pl.when(tile + NW >= q_tiles + 1)
        def _():
            first = (tile + NW - q_tiles - 1) * 2
            for g in range(2):
                for c in cache_in(first + g):
                    c.start()
        return carry

    lax.fori_loop(0, q_tiles, q_step, 0)
    out = qkv_tile(q_tiles)
    for g in range(2):
        for c in cache_in((NW - 1) * 2 + g):
            c.start()
    for g in range(2):
        kn[g] = rope(out[:, g * HEAD_DIM:(g + 1) * HEAD_DIM])
        vn[g] = out[:, (2 + g) * HEAD_DIM:(3 + g) * HEAD_DIM]
    for hd in range(heads):
        qs[:, hd, :] = qh[hd]

    sub = lax.broadcasted_iota(jnp.int32, (16, HEAD_DIM), 0)
    scale = HEAD_DIM ** -0.5

    def group_step(group, carry):
        slot = lax.rem(group, NS)
        for c in cache_in(group):
            c.wait()
        for j in range(SG):
            seq = group * SG + j
            length = len_ref[seq]
            start = pl.multiple_of((length // 8) * 16, 16)
            here = (sub >> 1) == (length - (length // 8) * 8)
            for buf, new in ((kbuf, kn), (vbuf, vn)):
                pattern = jnp.where((sub & 1) == 0, new[0, pl.ds(seq, 1), :], new[1, pl.ds(seq, 1), :])
                old = buf[slot, j, pl.ds(start, 16), :].astype(F32)
                buf[slot, j, pl.ds(start, 16), :] = jnp.where(here, pattern, old).astype(BF16)
        for c in cache_out(group):
            c.start()
        dims = (((1,), (1,)), ((), ()))
        seqs = [group * SG + j for j in range(SG)]
        scores = [lax.dot_general(qs[seqs[j]].astype(BF16), kbuf[slot, j], dims, preferred_element_type=F32) * scale
                  for j in range(SG)]
        scores = [jnp.where(colpos[...] <= len_ref[seqs[j]], scores[j], -jnp.inf) for j in range(SG)]
        tops = [jnp.max(v, axis=-1, keepdims=True) for v in scores]
        weights = [jnp.exp(v - t) for v, t in zip(scores, tops)]
        totals = [jnp.sum(v, axis=-1, keepdims=True) for v in weights]
        probs = [(v / t).astype(BF16) for v, t in zip(weights, totals)]
        for j in range(SG):
            cb[seqs[j]] = jnp.dot(probs[j], vbuf[slot, j], preferred_element_type=F32)

        @pl.when(group >= LAG)
        def _():
            for c in cache_out(group - LAG):
                c.wait()

        @pl.when(jnp.logical_and(group >= LAG, group - LAG + NS < groups))
        def _():
            for c in cache_in(group - LAG + NS):
                c.start()

        return carry

    lax.fori_loop(0, groups, group_step, 0)
    for hd in range(heads):
        ctx_ref[:, hd * HEAD_DIM:(hd + 1) * HEAD_DIM] = cb[:, hd, :].astype(BF16)
    for g in range(LAG):
        for c in cache_out(groups - LAG + g):
            c.wait()


def attention_block(x_in, seq_len, k_cache, v_cache, gamma_attn, w_qkv, b_qkv):
    rows, width = x_in.shape
    cache_len, kv_heads = k_cache.shape[1], k_cache.shape[2]
    q_width = w_qkv.shape[1] - 2 * kv_heads * HEAD_DIM
    heads = q_width // HEAD_DIM
    span = cache_len * kv_heads
    flat = (rows, span, HEAD_DIM)
    vmem = pl.BlockSpec(memory_space=pltpu.VMEM)
    hbm = pl.BlockSpec(memory_space=pl.ANY)
    ctx, k_out, v_out = pl.pallas_call(
        attention_kernel,
        out_shape=(jax.ShapeDtypeStruct((rows, q_width), BF16),
                   jax.ShapeDtypeStruct(flat, BF16), jax.ShapeDtypeStruct(flat, BF16)),
        in_specs=[pl.BlockSpec(memory_space=pltpu.SMEM)] + [vmem] * 3 + [hbm] * 3,
        out_specs=(vmem, hbm, hbm),
        scratch_shapes=[
            pltpu.VMEM((NW, width, TN), BF16),
            pltpu.VMEM((NS, SG, span, HEAD_DIM), BF16),
            pltpu.VMEM((NS, SG, span, HEAD_DIM), BF16),
            pltpu.VMEM((rows, width), BF16),
            pltpu.VMEM((1, w_qkv.shape[1]), F32),
            pltpu.VMEM((rows, HEAD_DIM), F32),
            pltpu.VMEM((rows, HEAD_DIM), F32),
            pltpu.VMEM((heads, rows, HEAD_DIM), F32),
            pltpu.VMEM((rows, heads, HEAD_DIM), F32),
            pltpu.VMEM((kv_heads, rows, HEAD_DIM), F32),
            pltpu.VMEM((kv_heads, rows, HEAD_DIM), F32),
            pltpu.VMEM((rows, heads, HEAD_DIM), F32),
            pltpu.VMEM((heads, span), jnp.int32),
            pltpu.SemaphoreType.DMA((NW,)),
            pltpu.SemaphoreType.DMA((NS, 2)),
            pltpu.SemaphoreType.DMA((NS, 2)),
        ],
        compiler_params=pltpu.CompilerParams(vmem_limit_bytes=56 * 1024 * 1024),
        name='attention_block',
    )(seq_len, x_in, gamma_attn, b_qkv, k_cache.reshape(flat), v_cache.reshape(flat), w_qkv)
    return ctx, k_out.reshape(k_cache.shape), v_out.reshape(v_cache.shape)


FT = 1024
HT = 256
RELAY_AT = 5


PT = 512
PSLOTS = 6
SHIFT = 2.0 ** 64


def mlp_kernel(ctx_in, x_in, gm_in, wp, wi, wo, out_ref,
               gs, rows_all, rs_all, wib, wob, gbuf, facc, hold, acc, topart, frompart, outbox,
               from_l, from_r, mid_l, mid_r,
               psem, wsem, osem, gsend, grecv, psend, precv, bsend, brecv):
    me = lax.axis_index('grp')
    chips = lax.axis_size('grp') // 2
    chip, core = me // 2, me % 2
    right = lax.rem(chip + 1, chips) * 2 + core
    left = lax.rem(chip + chips - 1, chips) * 2 + core
    partner = chip * 2 + 1 - core
    r = x_in.shape[0]
    s, g, br = r // 2, 2 * r, 4 * r
    hidden = wo.shape[0]
    full = hidden // HT
    rest = hidden - full * HT
    hpad = wob.shape[0]
    tiles = wo.shape[1] // FT

    def w_copy(j):
        part = pl.ds(pl.multiple_of(j * HT, HT), HT)
        return pltpu.make_async_copy(wi.at[:, part], wib.at[:, part], wsem.at[j])

    last_in = pltpu.make_async_copy(wi.at[:, pl.ds(full * HT, rest)], wib.at[:, pl.ds(full * HT, rest)], wsem.at[full])
    o_copy = pltpu.make_async_copy(wo, wob.at[pl.ds(0, hidden)], osem)
    p_tiles = wp.shape[1] // PT
    depth = wp.shape[0] // PT

    def p_part(t, k):
        slot = t % PSLOTS
        buf, row = (wob, slot * PT) if slot < PSLOTS // 2 else (wib.at[1], (slot - PSLOTS // 2) * PT)
        return buf.at[pl.ds(row, PT), pl.ds(k * PT, PT)]

    def p_copy(t, k):
        return pltpu.make_async_copy(wp.at[pl.ds(k * PT, PT), pl.ds(t * PT, PT)], p_part(t, k), psem.at[t % PSLOTS, k])

    for t in range(PSLOTS):
        for k in range(depth):
            p_copy(t, k).start()
    gs[...] = gm_in[...].astype(F32)[None, :] * (1.0 / SHIFT)

    barrier = pltpu.get_barrier_semaphore()
    for dev in (right, left, partner):
        pl.semaphore_signal(barrier, inc=1, device_id={'grp': dev}, device_id_type=pl.DeviceIdType.MESH)
    pl.semaphore_wait(barrier, 3)

    def remote(src, dst, send, recv, dev):
        return pltpu.make_async_remote_copy(src_ref=src, dst_ref=dst, send_sem=send, recv_sem=recv,
                                            device_id={'grp': dev}, device_id_type=pl.DeviceIdType.MESH)

    def gather(n, src, dst, count, dev):
        def at(c):
            def view(first):
                if c == tiles:
                    return rs_all.at[pl.ds(first, count)]
                return rows_all.at[pl.ds(first, count), pl.ds(c * FT, FT)]
            return remote(view(src), view(dst), gsend.at[n, c], grecv.at[n, c], dev)
        return at

    to_r0 = gather(0, 0, r, s, right)
    to_l1 = gather(1, s, r + s, s, left)
    to_r1 = gather(2, s, br + r, s, right)
    to_l0 = gather(3, 0, br + r + s, s, left)
    to_p = gather(4, 0, g, r, partner)
    on_r = gather(5, r, br, s, right)
    on_l = gather(6, r + s, br + s, s, left)
    p_l0 = gather(7, r, g + r, s, partner)
    p_r1 = gather(8, r + s, g + r + s, s, partner)
    p_l1 = gather(9, br + r, br + g + r, s, partner)
    p_r0 = gather(10, br + r + s, br + g + r + s, s, partner)
    p_o0 = gather(11, br, br + g, s, partner)
    p_o1 = gather(12, br + s, br + g + s, s, partner)
    gathers = [to_r0, to_l1, to_r1, to_l0, to_p, on_r, on_l, p_l0, p_r1, p_l1, p_r0, p_o0, p_o1]

    def give(c):
        for copy in (to_r0, to_l1, to_r1, to_l0, to_p):
            copy(c).start()

    def pass_on(c):
        to_r0(c).wait_recv()
        on_r(c).start()
        p_l0(c).start()
        to_l1(c).wait_recv()
        on_l(c).start()
        p_r1(c).start()
        to_r1(c).wait_recv()
        p_l1(c).start()
        to_l0(c).wait_recv()
        p_r0(c).start()

    def pass_far(c):
        on_r(c).wait_recv()
        p_o0(c).start()
        on_l(c).wait_recv()
        p_o1(c).start()

    if hpad > hidden:
        wib[:, hidden:, :] = jnp.zeros((2, hpad - hidden, wib.shape[2]), BF16)
        wob[hidden:, :] = jnp.zeros((hpad - hidden, wob.shape[1]), BF16)

    square = jnp.zeros((r, HEAD_DIM), F32)
    per = FT // PT
    for t in range(p_tiles):
        part = slice(t * PT, (t + 1) * PT)
        out = None
        for k in range(depth):
            p_copy(t, k).wait()
        for k in range(depth):
            term = jnp.dot(ctx_in[:, k * PT:(k + 1) * PT], p_part(t, k)[...], preferred_element_type=F32)
            out = term if out is None else out + term
        hid = x_in[:, part].astype(F32) + out
        acc[:, part] = hid
        rows_all[0:r, part] = (hid * gs[:, part]).astype(BF16)
        for k in range(PT // HEAD_DIM):
            lanes = hid[:, k * HEAD_DIM:(k + 1) * HEAD_DIM]
            square = square + lanes * lanes
        if t + PSLOTS < p_tiles:
            for k in range(depth):
                p_copy(t + PSLOTS, k).start()
        if t == PSLOTS - 1:
            for j in range(full):
                w_copy(j).start()
            if rest:
                last_in.start()
        if t % per == per - 1:
            give(t // per)
        if t == p_tiles - 3:
            pass_on(0)
    o_copy.start()
    mean_sq = jnp.sum(square, axis=-1, keepdims=True) / wp.shape[1]
    rs_all[0:r, :] = jnp.broadcast_to(lax.rsqrt(mean_sq + EPS) * SHIFT, (r, HEAD_DIM))
    give(tiles)
    for c in range(1, tiles + 1):
        pass_on(c)
        pass_far(c - 1)
    pass_far(tiles)
    for c in range(tiles + 1):
        for copy in (to_p, p_l0, p_r1, p_l1, p_r0, p_o0, p_o1):
            copy(c).wait_recv()

    def gate_tile(blk, j):
        part = pl.ds(pl.multiple_of(j * HT, HT), HT)
        x = rows_all[pl.ds(blk * br, br)]
        dims = (((1,), (1,)), ((), ()))
        gate = lax.dot_general(x, wib[0, part, :], dims, preferred_element_type=F32)
        up = lax.dot_general(x, wib[1, part, :], dims, preferred_element_type=F32)
        scale = rs_all[pl.ds(blk * br, br), 0:1]
        gate = jnp.where(scale > 0.0, gate * scale, 0.0)
        up = jnp.where(scale > 0.0, up * scale, 0.0)
        gbuf[:, part] = (jax.nn.silu(gate) * up).astype(BF16)

    def cols(t):
        return slice(t * FT, (t + 1) * FT)

    def to_partner(blk, t):
        return remote(topart.at[t], frompart.at[blk, t], psend.at[blk, t], precv.at[blk, t], partner)

    def out_copy(kind, t):
        dst = (from_r.at[0, t], from_l.at[1, t], mid_l.at[t], mid_r.at[t], from_l.at[0, t], from_r.at[1, t])[kind]
        dev = (left, right, right, left, right, left)[kind]
        return remote(outbox.at[kind, t], dst, bsend.at[kind, t], brecv.at[kind, t], dev)

    def post(kind, t, vals):
        outbox[kind, t] = vals.astype(BF16)
        out_copy(kind, t).start()

    def down_tile(blk, t):
        f = jnp.dot(gbuf[...], wob[:, cols(t)], preferred_element_type=F32)
        if blk == 0:
            to_partner(1, t).wait_send()
        topart[t] = f[g:].astype(BF16)
        to_partner(blk, t).start()
        facc[t % 2] = f[:g]

    def finish(blk, t):
        to_partner(blk, t).wait_recv()
        total = facc[t % 2] + frompart[blk, t].astype(F32)
        if blk == 0:
            acc[:, cols(t)] += total[:r]
            post(0, t, total[r:r + s])
            post(1, t, total[r + s:])
        else:
            post(2, t, total[:s])
            post(3, t, total[s:r])
            hold[t] = total[r:]

    def far_step(j, carry):
        w_copy(j).wait()
        gate_tile(1, j)
        return carry

    def near_step(j, carry):
        gate_tile(0, j)
        return carry

    lax.fori_loop(0, full, far_step, 0)
    if rest:
        last_in.wait()
        gate_tile(1, full)
    o_copy.wait()
    for t in range(tiles):
        down_tile(1, t)
        if t:
            finish(1, t - 1)
    gate_tile(0, 0)
    finish(1, tiles - 1)
    lax.fori_loop(1, RELAY_AT, near_step, 0)
    for t in range(tiles):
        out_copy(2, t).wait_recv()
        post(4, t, hold[t, s:] + mid_l[t].astype(F32))
        out_copy(3, t).wait_recv()
        post(5, t, hold[t, :s] + mid_r[t].astype(F32))
    lax.fori_loop(RELAY_AT, hpad // HT, near_step, 0)
    for t in range(tiles):
        down_tile(0, t)
        if t:
            finish(0, t - 1)
    finish(0, tiles - 1)
    for t in range(tiles):
        for kind in (0, 1, 4, 5):
            out_copy(kind, t).wait_recv()
        for half in range(2):
            part = slice(half * s, (half + 1) * s)
            total = acc[part, cols(t)] + (from_l[half, t].astype(F32) + from_r[half, t].astype(F32))
            out_ref[part, cols(t)] = total.astype(BF16)
    for copy in gathers:
        for c in range(tiles + 1):
            copy(c).wait_send()
    for t in range(tiles):
        to_partner(0, t).wait_send()
        for kind in range(6):
            out_copy(kind, t).wait_send()


def mlp_block(ctx, x_in, gamma_mlp, w_proj, w_in, w_out):
    rows, width = x_in.shape
    hidden = w_out.shape[0]
    hpad = -(-hidden // HT) * HT
    tiles = width // FT
    half, group, block = rows // 2, 2 * rows, 4 * rows
    hbm = pl.BlockSpec(memory_space=pl.ANY)
    vmem = pl.BlockSpec(memory_space=pltpu.VMEM)
    dma = pltpu.SemaphoreType.DMA
    return pl.pallas_call(
        mlp_kernel,
        out_shape=jax.ShapeDtypeStruct((rows, width), BF16),
        in_specs=[vmem] * 3 + [hbm] * 3,
        out_specs=vmem,
        scratch_shapes=[
            pltpu.VMEM((1, width), F32),
            pltpu.VMEM((2 * block, width), BF16),
            pltpu.VMEM((2 * block, HEAD_DIM), F32),
            pltpu.VMEM((2, hpad, width), BF16),
            pltpu.VMEM((hpad, width), BF16),
            pltpu.VMEM((block, hpad), BF16),
            pltpu.VMEM((2, group, FT), F32),
            pltpu.VMEM((tiles, rows, FT), F32),
            pltpu.VMEM((rows, width), F32),
            pltpu.VMEM((tiles, group, FT), BF16),
            pltpu.VMEM((2, tiles, group, FT), BF16),
            pltpu.VMEM((6, tiles, half, FT), BF16),
            pltpu.VMEM((2, tiles, half, FT), BF16),
            pltpu.VMEM((2, tiles, half, FT), BF16),
            pltpu.VMEM((tiles, half, FT), BF16),
            pltpu.VMEM((tiles, half, FT), BF16),
            dma((PSLOTS, w_proj.shape[0] // PT)), dma((hpad // HT,)), dma, dma((13, tiles + 1)), dma((13, tiles + 1)),
            dma((2, tiles)), dma((2, tiles)), dma((6, tiles)), dma((6, tiles)),
        ],
        compiler_params=pltpu.CompilerParams(vmem_limit_bytes=67043328, collective_id=0, has_side_effects=True),
        name='mlp_block',
    )(ctx, x_in, gamma_mlp, w_proj, w_in, w_out)


def solution(mesh):
    row_spec = P(('rep', 'grp'))
    repl_spec = P()

    def local_layer(x_in, seq_len, k_cache, v_cache, gamma_attn, w_qkv, b_qkv, w_proj, gamma_mlp, w_in, w_out):
        ctx, k_out, v_out = attention_block(x_in, seq_len, k_cache, v_cache, gamma_attn, w_qkv, b_qkv)
        layer_out = mlp_block(ctx, x_in, gamma_mlp, w_proj, w_in, w_out)
        return layer_out, k_out, v_out

    return jax.shard_map(local_layer, mesh=mesh,
                         in_specs=(row_spec, row_spec, row_spec, row_spec, repl_spec, repl_spec, repl_spec,
                                   repl_spec, repl_spec, P(None, 'grp', None), P('grp', None)),
                         out_specs=(row_spec, row_spec, row_spec), check_vma=False)
```

time: 122 us -> 107 us (0.88)
  Pallas kernels: 114 us -> 104 us
  local copies, waits for them, and re-layouts: 5.79 us -> 1.87 us
  other arithmetic: 1.5 us -> 0 us
    pallas_call x1, Pallas kernels: 54.2 us -> 35.6 us  [attention_block(): pl.pallas_call(attention_kernel, out_shape=(jax.ShapeDtypeStruct((rows, q...]
    pallas_call x1, Pallas kernels: 59.9 us -> 68.9 us  [mlp_block(): pl.pallas_call(mlp_kernel, out_shape=jax.ShapeDtypeStruct((rows, width),...]
    broadcast_in_dim x3 -> x0, local copies, waits for them, and re-layouts: 3.92 us -> none  [the longest x1 1.31 us: attention_block(): b_qkv[None, :]]
where the time goes in v3:
time: 107 us
  Pallas kernels  104 us (97%)
  local copies, waits for them, and re-layouts  1.87 us (2%)
    pallas_call x1, Pallas kernels, mlp_block(): pl.pallas_call(mlp_kernel, out_shape=jax.ShapeDtypeStruct((rows, width),...  68.9 us
    pallas_call x1, Pallas kernels, attention_block(): pl.pallas_call(attention_kernel, out_shape=(jax.ShapeDtypeStruct((rows, q...  35.6 us

profile of v3, /device:TPU:113, one launch (start us, length us, event | category | flops | bytes accessed | tf_op | source)
XLA Modules:
  0.0 107.0 jit_solution(8982993811778260679)
XLA Ops:
  0.6 35.6 %attention_block.1 = (bf16[64,4096]{1,0:T(8,128)(2,1)}, bf16[64,1024,128]{2,1,0:T(8,128)(2,1)}, bf16[64,1024,128]{2,1,0:T(8,128)(2,1)}) custom-call(s32[64]{0:T(128)} %len_ref.1, bf16[64,4096]{1,0:T(8,128)(2,1)} %x_in.1, bf16[4096]{0:T(1024)(128)(2,1)} %ga_ref.1, bf16[4608]{0:T(1024)(128)(2,1)} %b_ref.1, bf16[64,1024,128]{2,1,0:T(8,128)(2,1)} %bitcast.4, ...), custom_call_target="tpu_custom_call" | custom-call | tf_op jit(solution)/shard_map/attention_block/pallas_call | solution.py:176
  36.3 68.9 %mlp_block.1 = bf16[64,4096]{1,0:T(8,128)(2,1)} custom-call(bf16[64,4096]{1,0:T(8,128)(2,1)} %get-tuple-element.6.ctx_in, bf16[64,4096]{1,0:T(8,128)(2,1)} %x_in.1, bf16[4096]{0:T(1024)(128)(2,1)} %gm_in.1, bf16[4096,4096]{1,0:T(8,128)(2,1)} %wp.1, bf16[2,1712,4096]{2,1,0:T(8,128)(2,1)} %wi.1, bf16[1712,4096]{1,0:T(8,128)(2,1)} %wo.1), custom_call_target="tpu_custom_call" | custom-call | tf_op jit(solution)/shard_map/mlp_block/pallas_call | solution.py:458
  105.1 1.9 %copy.15 = bf16[64,4096]{1,0:T(8,128)(2,1)} copy(bf16[64,4096]{1,0:T(8,128)(2,1)} %mlp_block.1) | data formatting | bytes 1048576

commit v4 on v3

--- a/solution.py
+++ b/solution.py
@@ -205,16 +205,18 @@
 
 FT = 1024
 HT = 256
-RELAY_AT = 5
 
 
 PT = 512
 PSLOTS = 6
+AHEAD = 2
+HOP = 4
+FAR = 3
 SHIFT = 2.0 ** 64
 
 
 def mlp_kernel(ctx_in, x_in, gm_in, wp, wi, wo, out_ref,
-               gs, rows_all, rs_all, wib, wob, gbuf, facc, hold, acc, topart, frompart, outbox,
+               gs, rows_all, rs_all, wib, wob, gbuf, facc, acc, topart, frompart, outbox,
                from_l, from_r, mid_l, mid_r,
                psem, wsem, osem, gsend, grecv, psend, precv, bsend, brecv):
     me = lax.axis_index('grp')
@@ -248,7 +250,7 @@
     def p_copy(t, k):
         return pltpu.make_async_copy(wp.at[pl.ds(k * PT, PT), pl.ds(t * PT, PT)], p_part(t, k), psem.at[t % PSLOTS, k])
 
-    for t in range(PSLOTS):
+    for t in range(AHEAD):
         for k in range(depth):
             p_copy(t, k).start()
     gs[...] = gm_in[...].astype(F32)[None, :] * (1.0 / SHIFT)
@@ -265,38 +267,36 @@
     def gather(n, src, dst, count, dev):
         def at(c):
             def view(first):
-                if c == tiles:
+                if c == p_tiles:
                     return rs_all.at[pl.ds(first, count)]
-                return rows_all.at[pl.ds(first, count), pl.ds(c * FT, FT)]
+                return rows_all.at[pl.ds(first, count), pl.ds(c * PT, PT)]
             return remote(view(src), view(dst), gsend.at[n, c], grecv.at[n, c], dev)
         return at
 
-    to_r0 = gather(0, 0, r, s, right)
-    to_l1 = gather(1, s, r + s, s, left)
-    to_r1 = gather(2, s, br + r, s, right)
-    to_l0 = gather(3, 0, br + r + s, s, left)
-    to_p = gather(4, 0, g, r, partner)
-    on_r = gather(5, r, br, s, right)
-    on_l = gather(6, r + s, br + s, s, left)
+    to_r0 = gather(0, br, r, s, right)
+    to_l1 = gather(1, br + s, r + s, s, left)
+    to_r1 = gather(2, br + s, br + r, s, right)
+    to_l0 = gather(3, br, br + r + s, s, left)
+    to_p = gather(4, br, br + g, r, partner)
+    on_r = gather(5, r, 0, s, right)
+    on_l = gather(6, r + s, s, s, left)
     p_l0 = gather(7, r, g + r, s, partner)
     p_r1 = gather(8, r + s, g + r + s, s, partner)
     p_l1 = gather(9, br + r, br + g + r, s, partner)
     p_r0 = gather(10, br + r + s, br + g + r + s, s, partner)
-    p_o0 = gather(11, br, br + g, s, partner)
-    p_o1 = gather(12, br + s, br + g + s, s, partner)
+    p_o0 = gather(11, 0, g, s, partner)
+    p_o1 = gather(12, s, g + s, s, partner)
     gathers = [to_r0, to_l1, to_r1, to_l0, to_p, on_r, on_l, p_l0, p_r1, p_l1, p_r0, p_o0, p_o1]
 
-    def give(c):
-        for copy in (to_r0, to_l1, to_r1, to_l0, to_p):
-            copy(c).start()
-
-    def pass_on(c):
+    def pass_first(c):
         to_r0(c).wait_recv()
         on_r(c).start()
         p_l0(c).start()
         to_l1(c).wait_recv()
         on_l(c).start()
         p_r1(c).start()
+
+    def pass_second(c):
         to_r1(c).wait_recv()
         p_l1(c).start()
         to_l0(c).wait_recv()
@@ -313,43 +313,53 @@
         wob[hidden:, :] = jnp.zeros((hpad - hidden, wob.shape[1]), BF16)
 
     square = jnp.zeros((r, HEAD_DIM), F32)
-    per = FT // PT
     for t in range(p_tiles):
         part = slice(t * PT, (t + 1) * PT)
         out = None
         for k in range(depth):
             p_copy(t, k).wait()
+        if t + AHEAD < p_tiles:
+            for k in range(depth):
+                p_copy(t + AHEAD, k).start()
         for k in range(depth):
             term = jnp.dot(ctx_in[:, k * PT:(k + 1) * PT], p_part(t, k)[...], preferred_element_type=F32)
             out = term if out is None else out + term
         hid = x_in[:, part].astype(F32) + out
         acc[:, part] = hid
-        rows_all[0:r, part] = (hid * gs[:, part]).astype(BF16)
+        rows_all[br:br + r, part] = (hid * gs[:, part]).astype(BF16)
+        for copy in (to_r0, to_l1, to_p):
+            copy(t).start()
+        if t < HOP:
+            to_r1(t).start()
+            to_l0(t).start()
         for k in range(PT // HEAD_DIM):
             lanes = hid[:, k * HEAD_DIM:(k + 1) * HEAD_DIM]
             square = square + lanes * lanes
-        if t + PSLOTS < p_tiles:
-            for k in range(depth):
-                p_copy(t + PSLOTS, k).start()
-        if t == PSLOTS - 1:
-            for j in range(full):
-                w_copy(j).start()
-            if rest:
-                last_in.start()
-        if t % per == per - 1:
-            give(t // per)
-        if t == p_tiles - 3:
-            pass_on(0)
+        if t == p_tiles - 2:
+            w_copy(0).start()
+        if t >= HOP:
+            pass_first(t - HOP)
+            pass_second(t - HOP)
+        if t >= HOP + FAR:
+            pass_far(t - HOP - FAR)
+    for j in range(1, full):
+        w_copy(j).start()
+    if rest:
+        last_in.start()
     o_copy.start()
     mean_sq = jnp.sum(square, axis=-1, keepdims=True) / wp.shape[1]
-    rs_all[0:r, :] = jnp.broadcast_to(lax.rsqrt(mean_sq + EPS) * SHIFT, (r, HEAD_DIM))
-    give(tiles)
-    for c in range(1, tiles + 1):
-        pass_on(c)
-        pass_far(c - 1)
-    pass_far(tiles)
-    for c in range(tiles + 1):
-        for copy in (to_p, p_l0, p_r1, p_l1, p_r0, p_o0, p_o1):
+    rs_all[br:br + r, :] = jnp.broadcast_to(lax.rsqrt(mean_sq + EPS) * SHIFT, (r, HEAD_DIM))
+    for copy in (to_r0, to_l1, to_p):
+        copy(p_tiles).start()
+    for c in range(p_tiles - HOP, p_tiles + 1):
+        pass_first(c)
+        to_r1(c).start()
+        to_l0(c).start()
+        pass_far(c - FAR)
+    for c in range(p_tiles - FAR + 1, p_tiles + 1):
+        pass_far(c)
+    for c in range(p_tiles + 1):
+        for copy in (p_l0, p_r1, p_o0, p_o1):
             copy(c).wait_recv()
 
     def gate_tile(blk, j):
@@ -380,56 +390,59 @@
 
     def down_tile(blk, t):
         f = jnp.dot(gbuf[...], wob[:, cols(t)], preferred_element_type=F32)
-        if blk == 0:
-            to_partner(1, t).wait_send()
+        if blk == 1:
+            to_partner(0, t).wait_send()
         topart[t] = f[g:].astype(BF16)
         to_partner(blk, t).start()
-        facc[t % 2] = f[:g]
+        facc[t % 3] = f[:g]
 
     def finish(blk, t):
         to_partner(blk, t).wait_recv()
-        total = facc[t % 2] + frompart[blk, t].astype(F32)
+        total = facc[t % 3] + frompart[blk, t].astype(F32)
         if blk == 0:
-            acc[:, cols(t)] += total[:r]
+            post(2, t, total[:s])
+            post(3, t, total[s:r])
             post(0, t, total[r:r + s])
             post(1, t, total[r + s:])
         else:
-            post(2, t, total[:s])
-            post(3, t, total[s:r])
-            hold[t] = total[r:]
-
-    def far_step(j, carry):
+            acc[:, cols(t)] += total[:r]
+            out_copy(2, t).wait_recv()
+            post(4, t, total[r + s:] + mid_l[t].astype(F32))
+            out_copy(3, t).wait_recv()
+            post(5, t, total[r:r + s] + mid_r[t].astype(F32))
+
+    def first_step(j, carry):
         w_copy(j).wait()
+        gate_tile(0, j)
+        return carry
+
+    def second_step(j, carry):
         gate_tile(1, j)
         return carry
 
-    def near_step(j, carry):
-        gate_tile(0, j)
-        return carry
-
-    lax.fori_loop(0, full, far_step, 0)
+    lax.fori_loop(0, full, first_step, 0)
     if rest:
         last_in.wait()
-        gate_tile(1, full)
+        gate_tile(0, full)
+    for c in range(HOP, p_tiles + 1):
+        pass_second(c)
     o_copy.wait()
+    for t in range(tiles):
+        down_tile(0, t)
+        if t >= 2:
+            finish(0, t - 2)
+    finish(0, tiles - 2)
+    for c in range(p_tiles + 1):
+        for copy in (to_p, p_l1, p_r0):
+            copy(c).wait_recv()
+    gate_tile(1, 0)
+    finish(0, tiles - 1)
+    lax.fori_loop(1, hpad // HT, second_step, 0)
     for t in range(tiles):
         down_tile(1, t)
         if t:
             finish(1, t - 1)
-    gate_tile(0, 0)
     finish(1, tiles - 1)
-    lax.fori_loop(1, RELAY_AT, near_step, 0)
-    for t in range(tiles):
-        out_copy(2, t).wait_recv()
-        post(4, t, hold[t, s:] + mid_l[t].astype(F32))
-        out_copy(3, t).wait_recv()
-        post(5, t, hold[t, :s] + mid_r[t].astype(F32))
-    lax.fori_loop(RELAY_AT, hpad // HT, near_step, 0)
-    for t in range(tiles):
-        down_tile(0, t)
-        if t:
-            finish(0, t - 1)
-    finish(0, tiles - 1)
     for t in range(tiles):
         for kind in (0, 1, 4, 5):
             out_copy(kind, t).wait_recv()
@@ -438,10 +451,10 @@
             total = acc[part, cols(t)] + (from_l[half, t].astype(F32) + from_r[half, t].astype(F32))
             out_ref[part, cols(t)] = total.astype(BF16)
     for copy in gathers:
-        for c in range(tiles + 1):
+        for c in range(p_tiles + 1):
             copy(c).wait_send()
     for t in range(tiles):
-        to_partner(0, t).wait_send()
+        to_partner(1, t).wait_send()
         for kind in range(6):
             out_copy(kind, t).wait_send()
 
@@ -467,8 +480,7 @@
             pltpu.VMEM((2, hpad, width), BF16),
             pltpu.VMEM((hpad, width), BF16),
             pltpu.VMEM((block, hpad), BF16),
-            pltpu.VMEM((2, group, FT), F32),
-            pltpu.VMEM((tiles, rows, FT), F32),
+            pltpu.VMEM((3, group, FT), F32),
             pltpu.VMEM((rows, width), F32),
             pltpu.VMEM((tiles, group, FT), BF16),
             pltpu.VMEM((2, tiles, group, FT), BF16),
@@ -477,7 +489,7 @@
             pltpu.VMEM((2, tiles, half, FT), BF16),
             pltpu.VMEM((tiles, half, FT), BF16),
             pltpu.VMEM((tiles, half, FT), BF16),
-            dma((PSLOTS, w_proj.shape[0] // PT)), dma((hpad // HT,)), dma, dma((13, tiles + 1)), dma((13, tiles + 1)),
+            dma((PSLOTS, w_proj.shape[0] // PT)), dma((hpad // HT,)), dma, dma((13, width // PT + 1)), dma((13, width // PT + 1)),
             dma((2, tiles)), dma((2, tiles)), dma((6, tiles)), dma((6, tiles)),
         ],
         compiler_params=pltpu.CompilerParams(vmem_limit_bytes=67043328, collective_id=0, has_side_effects=True),

time: 107 us -> 104 us (0.972)
  Pallas kernels: 104 us -> 101 us
    pallas_call x1, Pallas kernels: 68.9 us -> 65.9 us  [mlp_block(): pl.pallas_call(mlp_kernel, out_shape=jax.ShapeDtypeStruct((rows, width),...]
where the time goes in v4:
time: 104 us
  Pallas kernels  101 us (97%)
  local copies, waits for them, and re-layouts  1.87 us (2%)
    pallas_call x1, Pallas kernels, mlp_block(): pl.pallas_call(mlp_kernel, out_shape=jax.ShapeDtypeStruct((rows, width),...  65.9 us
    pallas_call x1, Pallas kernels, attention_block(): pl.pallas_call(attention_kernel, out_shape=(jax.ShapeDtypeStruct((rows, q...  35.6 us

profile of v4, /device:TPU:113, one launch (start us, length us, event | category | flops | bytes accessed | tf_op | source)
XLA Modules:
  0.0 104.0 jit_solution(15417582956998676737)
XLA Ops:
  0.6 35.6 %attention_block.1 = (bf16[64,4096]{1,0:T(8,128)(2,1)}, bf16[64,1024,128]{2,1,0:T(8,128)(2,1)}, bf16[64,1024,128]{2,1,0:T(8,128)(2,1)}) custom-call(s32[64]{0:T(128)} %len_ref.1, bf16[64,4096]{1,0:T(8,128)(2,1)} %x_in.1, bf16[4096]{0:T(1024)(128)(2,1)} %ga_ref.1, bf16[4608]{0:T(1024)(128)(2,1)} %b_ref.1, bf16[64,1024,128]{2,1,0:T(8,128)(2,1)} %bitcast.4, ...), custom_call_target="tpu_custom_call" | custom-call | tf_op jit(solution)/shard_map/attention_block/pallas_call | solution.py:176
  36.3 65.9 %mlp_block.1 = bf16[64,4096]{1,0:T(8,128)(2,1)} custom-call(bf16[64,4096]{1,0:T(8,128)(2,1)} %get-tuple-element.6.ctx_in, bf16[64,4096]{1,0:T(8,128)(2,1)} %x_in.1, bf16[4096]{0:T(1024)(128)(2,1)} %gm_in.1, bf16[4096,4096]{1,0:T(8,128)(2,1)} %wp.1, bf16[2,1712,4096]{2,1,0:T(8,128)(2,1)} %wi.1, bf16[1712,4096]{1,0:T(8,128)(2,1)} %wo.1), custom_call_target="tpu_custom_call" | custom-call | tf_op jit(solution)/shard_map/mlp_block/pallas_call | solution.py:471
  102.1 1.9 %copy.15 = bf16[64,4096]{1,0:T(8,128)(2,1)} copy(bf16[64,4096]{1,0:T(8,128)(2,1)} %mlp_block.1) | data formatting | bytes 1048576

commit v5 on v4

--- a/solution.py
+++ b/solution.py
@@ -210,7 +210,7 @@
 PT = 512
 PSLOTS = 6
 AHEAD = 2
-HOP = 4
+HOP = 3
 FAR = 3
 SHIFT = 2.0 ** 64
 
@@ -339,23 +339,26 @@
             w_copy(0).start()
         if t >= HOP:
             pass_first(t - HOP)
-            pass_second(t - HOP)
+            if t - HOP < HOP:
+                pass_second(t - HOP)
         if t >= HOP + FAR:
             pass_far(t - HOP - FAR)
-    for j in range(1, full):
-        w_copy(j).start()
-    if rest:
-        last_in.start()
-    o_copy.start()
+    loads = [w_copy(j) for j in range(1, full)] + ([last_in] if rest else []) + [o_copy]
     mean_sq = jnp.sum(square, axis=-1, keepdims=True) / wp.shape[1]
     rs_all[br:br + r, :] = jnp.broadcast_to(lax.rsqrt(mean_sq + EPS) * SHIFT, (r, HEAD_DIM))
     for copy in (to_r0, to_l1, to_p):
         copy(p_tiles).start()
     for c in range(p_tiles - HOP, p_tiles + 1):
+        for copy in loads[:2]:
+            copy.start()
+        loads = loads[2:]
         pass_first(c)
+        pass_far(c - FAR)
+    for copy in loads:
+        copy.start()
+    for c in range(HOP, p_tiles + 1):
         to_r1(c).start()
         to_l0(c).start()
-        pass_far(c - FAR)
     for c in range(p_tiles - FAR + 1, p_tiles + 1):
         pass_far(c)
     for c in range(p_tiles + 1):
@@ -424,7 +427,7 @@
     if rest:
         last_in.wait()
         gate_tile(0, full)
-    for c in range(HOP, p_tiles + 1):
+    for c in range(min(HOP, p_tiles - HOP), p_tiles + 1):
         pass_second(c)
     o_copy.wait()
     for t in range(tiles):
@@ -470,7 +473,7 @@
     dma = pltpu.SemaphoreType.DMA
     return pl.pallas_call(
         mlp_kernel,
-        out_shape=jax.ShapeDtypeStruct((rows, width), BF16),
+        out_shape=pltpu.VMEM((rows, width), BF16),
         in_specs=[vmem] * 3 + [hbm] * 3,
         out_specs=vmem,
         scratch_shapes=[
@@ -492,7 +495,7 @@
             dma((PSLOTS, w_proj.shape[0] // PT)), dma((hpad // HT,)), dma, dma((13, width // PT + 1)), dma((13, width // PT + 1)),
             dma((2, tiles)), dma((2, tiles)), dma((6, tiles)), dma((6, tiles)),
         ],
-        compiler_params=pltpu.CompilerParams(vmem_limit_bytes=67043328, collective_id=0, has_side_effects=True),
+        compiler_params=pltpu.CompilerParams(vmem_limit_bytes=60 * 1024 * 1024, collective_id=0, has_side_effects=True),
         name='mlp_block',
     )(ctx, x_in, gamma_mlp, w_proj, w_in, w_out)
 

time: 104 us -> 101 us (0.971)
  Pallas kernels: 101 us -> 99 us
  local copies, waits for them, and re-layouts: 1.87 us -> 0.8 us
    pallas_call x1, Pallas kernels: 65.9 us -> 63.5 us  [mlp_block(): pl.pallas_call(mlp_kernel, out_shape=pltpu.VMEM((rows, width), BF16), in_...]
    unnamed x1, local copies, waits for them, and re-layouts: 1.87 us -> 0.8 us
where the time goes in v5:
time: 101 us; the launch traced here: 100 us
  Pallas kernels  99 us (98%)
    pallas_call x1, Pallas kernels, mlp_block(): pl.pallas_call(mlp_kernel, out_shape=pltpu.VMEM((rows, width), BF16), in_...  63.5 us
    pallas_call x1, Pallas kernels, attention_block(): pl.pallas_call(attention_kernel, out_shape=(jax.ShapeDtypeStruct((rows, q...  35.6 us

profile of v5, /device:TPU:113, one launch (start us, length us, event | category | flops | bytes accessed | tf_op | source)
XLA Modules:
  0.0 100.5 jit_solution(15614831038793879523)
XLA Ops:
  0.6 35.6 %attention_block.1 = (bf16[64,4096]{1,0:T(8,128)(2,1)}, bf16[64,1024,128]{2,1,0:T(8,128)(2,1)}, bf16[64,1024,128]{2,1,0:T(8,128)(2,1)}) custom-call(s32[64]{0:T(128)} %len_ref.1, bf16[64,4096]{1,0:T(8,128)(2,1)} %x_in.1, bf16[4096]{0:T(1024)(128)(2,1)} %ga_ref.1, bf16[4608]{0:T(1024)(128)(2,1)} %b_ref.1, bf16[64,1024,128]{2,1,0:T(8,128)(2,1)} %bitcast.4, ...), custom_call_target="tpu_custom_call" | custom-call | tf_op jit(solution)/shard_map/attention_block/pallas_call | solution.py:176
  36.2 63.5 %mlp_block.1 = bf16[64,4096]{1,0:T(8,128)(2,1)S(1)} custom-call(bf16[64,4096]{1,0:T(8,128)(2,1)} %get-tuple-element.6.ctx_in, bf16[64,4096]{1,0:T(8,128)(2,1)} %x_in.1, bf16[4096]{0:T(1024)(128)(2,1)} %gm_in.1, bf16[4096,4096]{1,0:T(8,128)(2,1)} %wp.1, bf16[2,1712,4096]{2,1,0:T(8,128)(2,1)} %wi.1, bf16[1712,4096]{1,0:T(8,128)(2,1)} %wo.1), custom_call_target="tpu_custom_call" | custom-call | tf_op jit(solution)/shard_map/mlp_block/pallas_call | solution.py:474
  99.7 0.8 copy.15

commit v6 on v5

--- a/solution.py
+++ b/solution.py
@@ -175,7 +175,7 @@
     hbm = pl.BlockSpec(memory_space=pl.ANY)
     ctx, k_out, v_out = pl.pallas_call(
         attention_kernel,
-        out_shape=(jax.ShapeDtypeStruct((rows, q_width), BF16),
+        out_shape=(pltpu.VMEM((rows, q_width), BF16),
                    jax.ShapeDtypeStruct(flat, BF16), jax.ShapeDtypeStruct(flat, BF16)),
         in_specs=[pl.BlockSpec(memory_space=pltpu.SMEM)] + [vmem] * 3 + [hbm] * 3,
         out_specs=(vmem, hbm, hbm),
@@ -506,6 +506,7 @@
 
     def local_layer(x_in, seq_len, k_cache, v_cache, gamma_attn, w_qkv, b_qkv, w_proj, gamma_mlp, w_in, w_out):
         ctx, k_out, v_out = attention_block(x_in, seq_len, k_cache, v_cache, gamma_attn, w_qkv, b_qkv)
+        ctx = pltpu.with_memory_space_constraint(ctx, pltpu.VMEM)
         layer_out = mlp_block(ctx, x_in, gamma_mlp, w_proj, w_in, w_out)
         return layer_out, k_out, v_out
 

time: 101 us -> 99.7 us (0.987)
  no operation moved by 1% of the time
where the time goes in v6:
time: 99.7 us; the launch traced here: 99.5 us
  Pallas kernels  98.1 us (98%)
    pallas_call x1, Pallas kernels, mlp_block(): pl.pallas_call(mlp_kernel, out_shape=pltpu.VMEM((rows, width), BF16), in_...  63.3 us
    pallas_call x1, Pallas kernels, attention_block(): pl.pallas_call(attention_kernel, out_shape=(pltpu.VMEM((rows, q_width), B...  34.8 us

profile of v6, /device:TPU:113, one launch (start us, length us, event | category | flops | bytes accessed | tf_op | source)
XLA Modules:
  0.0 99.5 jit_solution(5706400695287469033)
XLA Ops:
  0.6 34.8 %attention_block.1 = (bf16[64,4096]{1,0:T(8,128)(2,1)S(1)}, bf16[64,1024,128]{2,1,0:T(8,128)(2,1)}, bf16[64,1024,128]{2,1,0:T(8,128)(2,1)}) custom-call(s32[64]{0:T(128)} %len_ref.1, bf16[64,4096]{1,0:T(8,128)(2,1)} %x_in.1, bf16[4096]{0:T(1024)(128)(2,1)} %ga_ref.1, bf16[4608]{0:T(1024)(128)(2,1)} %b_ref.1, bf16[64,1024,128]{2,1,0:T(8,128)(2,1)} %bitcast.4, ...), custom_call_target="tpu_custom_call" | custom-call | tf_op jit(solution)/shard_map/attention_block/pallas_call | solution.py:176
  35.5 63.3 %mlp_block.1 = bf16[64,4096]{1,0:T(8,128)(2,1)S(1)} custom-call(bf16[64,4096]{1,0:T(8,128)(2,1)S(1)} %get-tuple-element.6.ctx_in, bf16[64,4096]{1,0:T(8,128)(2,1)} %x_in.1, bf16[4096]{0:T(1024)(128)(2,1)} %gm_in.1, bf16[4096,4096]{1,0:T(8,128)(2,1)} %wp.1, bf16[2,1712,4096]{2,1,0:T(8,128)(2,1)} %wi.1, bf16[1712,4096]{1,0:T(8,128)(2,1)} %wo.1), custom_call_target="tpu_custom_call" | custom-call | tf_op jit(solution)/shard_map/mlp_block/pallas_call | solution.py:474
  98.7 0.8 copy.15
